TPU v7x, 32 devices: a whole 2x2x4 slice. The times are simulated.
32 devices in a mesh: scan: 16 (over z, x, core), tile: 2 (over y).
Axes of the slice: x: 2, y: 2, z: 4, core: 2. Of those that a mesh axis runs over, the one named last changes fastest.
Arguments:
- probe_modes: float32 [12, 2, 128, 128], replicated, may hold values from -5 to 5
- patterns: float32 [128, 128, 128], P(('scan', 'tile')), may hold values from 0.005 to 300
- specimen: float32 [2, 2048, 512], P(None, 'scan', 'tile'), may hold values from -17.5 to 17.5
- offsets: int32 [128, 2], P(('scan', 'tile')), may hold values from -128 to 2048, as said below
Outputs:
- new_probe: float32 [12, 2, 128, 128], replicated
- new_specimen: float32 [2, 2048, 512], P(None, 'scan', 'tile')
Inputs may be any that keep to these rules, and one draw needn't show every extreme that they name: `offsets`: position p lies in aligned block b = p // 4, held by the device of scan index s = b // (the number of tile devices) and tile index t = b % (the number of tile devices); its row offset lies in s * 128 - 128 to s * 128 + 128, its column offset in t * 256 - 128 to t * 256 + 256, both ends included; in every block one position has its row offset at the lower end and its column offset at the upper end, and one has its row offset at the upper end.
All inputs are finite; a program needn't handle non-finite values.
Results may differ from a plain program's by a relative error of at most 0.0001.
Values sent between devices are 32-bit elements; how exact they have to be, the bound alone decides.
A program may use at most 64 MiB of HBM per device.

v0:
```python
import math

import jax
import jax.numpy as jnp
from jax import lax
from jax.sharding import PartitionSpec as P

NS_STEPS = 8


highest = lax.Precision.HIGHEST
light_floor = 0.05
object_reg = 0.5
probe_reg = 1.0
total_eps = 1e-06


def extended_2(array, sides, width):
    for axis, dim in sides:
        size, length = (lax.axis_size(axis), array.shape[dim])
        up = [(i, (i + 1) % size) for i in range(size - 1)]
        down = [(j, i) for i, j in up]
        last = lax.slice_in_dim(array, length - width, length, axis=dim)
        first = lax.slice_in_dim(array, 0, width, axis=dim)
        before = lax.ppermute(last, axis, up)
        after = lax.ppermute(first, axis, down)
        array = jnp.concatenate([before, array, after], axis=dim)
    return array


def dft_tables(detector):
    indices = jnp.arange(detector, dtype=jnp.int32)
    product = indices[:, None] * indices[None, :] % detector
    angles = -2.0 * math.pi / detector * product.astype(jnp.float32)
    norm_factor = 1.0 / math.sqrt(detector)
    return (jnp.cos(angles) * norm_factor, jnp.sin(angles) * norm_factor)


def complex_section(real_part, imag_part, table, direction, on_right):
    stacked = jnp.stack([real_part, imag_part])
    if on_right:
        products = jnp.einsum(
            "cmxy,yw->cmxw", stacked, table, precision=highest, preferred_element_type=jnp.float32
        )
        split_at = real_part.shape[-1]
        plain_re, twist_re = (products[0, :, :, :split_at], products[0, :, :, split_at:])
        plain_im, twist_im = (products[1, :, :, :split_at], products[1, :, :, split_at:])
    else:
        products = jnp.einsum(
            "wx,cmxy->cmwy", table, stacked, precision=highest, preferred_element_type=jnp.float32
        )
        split_at = real_part.shape[-2]
        plain_re, twist_re = (products[0, :, :split_at], products[0, :, split_at:])
        plain_im, twist_im = (products[1, :, :split_at], products[1, :, split_at:])
    return (plain_re - direction * twist_im, direction * twist_re + plain_im)


def newton_steps(gram_re, gram_im):
    mode_count = gram_re.shape[0]
    upper = jnp.concatenate([gram_re, -gram_im], axis=1)
    lower = jnp.concatenate([gram_im, gram_re], axis=1)
    embedded = jnp.concatenate([upper, lower], axis=0)
    frobenius = jnp.sqrt(jnp.sum(embedded * embedded))
    identity = jnp.eye(2 * mode_count, dtype=jnp.float32)
    current = embedded / frobenius
    inverse = identity
    for repeat in range(NS_STEPS):
        factor = 1.5 * identity - 0.5 * jnp.dot(
            inverse, current, precision=highest, preferred_element_type=jnp.float32
        )
        current = jnp.dot(current, factor, precision=highest, preferred_element_type=jnp.float32)
        inverse = jnp.dot(factor, inverse, precision=highest, preferred_element_type=jnp.float32)
    inverse = inverse / jnp.sqrt(frobenius)
    return (inverse[:mode_count, :mode_count], inverse[mode_count:, :mode_count])


def gram_parts(mode_rows):
    real_rows = mode_rows[0::2]
    imag_rows = mode_rows[1::2]
    gram_re = jnp.dot(
        real_rows, real_rows.T, precision=highest, preferred_element_type=jnp.float32
    ) + jnp.dot(imag_rows, imag_rows.T, precision=highest, preferred_element_type=jnp.float32)
    gram_im = jnp.dot(
        real_rows, imag_rows.T, precision=highest, preferred_element_type=jnp.float32
    ) - jnp.dot(imag_rows, real_rows.T, precision=highest, preferred_element_type=jnp.float32)
    return (gram_re, gram_im)


def orthonormal_rows(mode_rows, gram_re, gram_im, power_ratio):
    real_rows = mode_rows[0::2]
    imag_rows = mode_rows[1::2]
    mix_re, mix_im = newton_steps(gram_re, gram_im)
    ortho_re = jnp.dot(
        mix_re.T, real_rows, precision=highest, preferred_element_type=jnp.float32
    ) - jnp.dot(mix_im.T, imag_rows, precision=highest, preferred_element_type=jnp.float32)
    ortho_im = jnp.dot(
        mix_im.T, real_rows, precision=highest, preferred_element_type=jnp.float32
    ) + jnp.dot(mix_re.T, imag_rows, precision=highest, preferred_element_type=jnp.float32)
    weight = jnp.sqrt(power_ratio * jnp.diagonal(gram_re))
    joined = jnp.stack([ortho_re, ortho_im], axis=1) * weight[:, None, None]
    return joined.reshape(mode_rows.shape)


def global_totals(measured, modeled):
    return lax.psum((measured, modeled), ("scan", "tile"))


def fold_interior(frame_sum, folded, detector, block_rows, block_cols):
    rows_end = block_rows + 3 * detector
    cols_end = block_cols + 3 * detector
    centre_rows = slice(2 * detector, 2 * detector + block_rows)
    centre_cols = slice(2 * detector, 2 * detector + block_cols)
    interior = frame_sum[:, detector : detector + block_rows, detector : detector + block_cols]
    interior = interior.at[:, :detector, :].add(folded[:, :detector, centre_cols])
    interior = interior.at[:, block_rows - detector :, :].add(folded[:, rows_end:, centre_cols])
    interior = interior.at[:, :, :detector].add(folded[:, centre_rows, :detector])
    interior = interior.at[:, :, block_cols - detector :].add(folded[:, centre_rows, cols_end:])
    interior = interior.at[:, :detector, :detector].add(folded[:, :detector, :detector])
    interior = interior.at[:, :detector, block_cols - detector :].add(
        folded[:, :detector, cols_end:]
    )
    interior = interior.at[:, block_rows - detector :, :detector].add(
        folded[:, rows_end:, :detector]
    )
    interior = interior.at[:, block_rows - detector :, block_cols - detector :].add(
        folded[:, rows_end:, cols_end:]
    )
    return interior


def body(probe_modes, patterns, specimen, offsets):
    detector = probe_modes.shape[-1]
    mode_count = probe_modes.shape[0]
    block_rows = specimen.shape[1]
    block_cols = specimen.shape[2]
    position_count = patterns.shape[0]
    table_re, table_im = dft_tables(detector)
    right_table = jnp.concatenate([table_re, table_im], axis=1)
    left_table = jnp.concatenate([table_re, table_im], axis=0)
    probe_re = probe_modes[:, 0]
    probe_im = probe_modes[:, 1]
    probe_power = jnp.sum(probe_re * probe_re + probe_im * probe_im, axis=0)
    extended = extended_2(specimen, (("scan", 1), ("tile", 2)), detector)
    row_base = lax.axis_index("scan") * block_rows - detector
    col_base = lax.axis_index("tile") * block_cols - detector
    local_rows = offsets[:, 0] - row_base
    local_cols = offsets[:, 1] - col_base
    zero_index = jnp.zeros((), jnp.int32)
    channels = 3

    def patch_at(position):
        return lax.dynamic_slice(
            extended,
            (zero_index, local_rows[position], local_cols[position]),
            (2, detector, detector),
        )

    def one_position(position, running):
        grad_re, grad_im, light_sum, frame_sum, model_sum = running
        patch_now = patch_at(position)
        patch_re = patch_now[0]
        patch_im = patch_now[1]
        exit_re = probe_re * patch_re[None] - probe_im * patch_im[None]
        exit_im = probe_re * patch_im[None] + probe_im * patch_re[None]
        model_sum = model_sum + jnp.sum(exit_re * exit_re + exit_im * exit_im)
        half_re, half_im = complex_section(exit_re, exit_im, right_table, 1.0, True)
        far_re, far_im = complex_section(half_re, half_im, left_table, 1.0, False)
        model_light = jnp.sum(far_re * far_re + far_im * far_im, axis=0)
        factor = (
            jnp.sqrt(patterns[position]) / jnp.sqrt(jnp.maximum(model_light, light_floor)) - 1.0
        )
        back_re, back_im = complex_section(
            far_re * factor[None], far_im * factor[None], right_table, -1.0, True
        )
        change_re, change_im = complex_section(back_re, back_im, left_table, -1.0, False)
        grad_re = grad_re + patch_re[None] * change_re + patch_im[None] * change_im
        grad_im = grad_im + patch_re[None] * change_im - patch_im[None] * change_re
        light_sum = light_sum + patch_re * patch_re + patch_im * patch_im
        num_re = jnp.sum(probe_re * change_re + probe_im * change_im, axis=0)
        num_im = jnp.sum(probe_re * change_im - probe_im * change_re, axis=0)
        addition = jnp.stack([num_re, num_im, probe_power])
        row_at = local_rows[position]
        col_at = local_cols[position]
        previous = lax.dynamic_slice(
            frame_sum, (zero_index, row_at, col_at), (channels, detector, detector)
        )
        frame_sum = lax.dynamic_update_slice(
            frame_sum, previous + addition, (zero_index, row_at, col_at)
        )
        return (grad_re, grad_im, light_sum, frame_sum, model_sum)

    mode_zeros = jnp.zeros((mode_count, detector, detector), jnp.float32)
    frame_init = jnp.zeros(
        (channels, block_rows + 2 * detector, block_cols + 2 * detector), jnp.float32
    )
    initial = (
        mode_zeros,
        mode_zeros,
        jnp.zeros((detector, detector), jnp.float32),
        frame_init,
        jnp.zeros((), jnp.float32),
    )
    grad_re, grad_im, light_sum, frame_sum, model_sum = lax.fori_loop(
        0, position_count, one_position, initial
    )
    measured_all, model_all = global_totals(jnp.sum(patterns), model_sum)
    power_ratio = measured_all / (model_all + total_eps)
    folded = extended_2(frame_sum, (("scan", 1), ("tile", 2)), detector)
    interior = fold_interior(frame_sum, folded, detector, block_rows, block_cols)
    interior_num = interior[0:2]
    interior_light = interior[2]
    new_specimen = specimen + interior_num / (interior_light + object_reg)[None]
    grad_rows = jnp.stack([grad_re, grad_im], axis=1).reshape(2 * mode_count, -1)
    light_row = light_sum.reshape(1, -1)
    probe_rows = probe_modes.reshape(2 * mode_count, -1)
    grad_total, light_total = lax.psum((grad_rows, light_row), ("scan", "tile"))
    updated = probe_rows + grad_total / (light_total + probe_reg)
    gram_re, gram_im = gram_parts(updated)
    new_probe = orthonormal_rows(updated, gram_re, gram_im, power_ratio).reshape(probe_modes.shape)
    return (new_probe, new_specimen)


def solution(mesh):
    return jax.shard_map(
        body,
        mesh=mesh,
        in_specs=(
            P(),
            P(("scan", "tile"), None, None),
            P(None, "scan", "tile"),
            P(("scan", "tile"), None),
        ),
        out_specs=(P(), P(None, "scan", "tile")),
        check_vma=False,
    )
```

profile of v0, /device:TPU:0, one launch (start us, length us, event | category | flops | bytes accessed | tf_op | source)
XLA Modules:
  0.0 348.0 jit_solution(15075586222732396307)
XLA Ops:
  8.7 3.1 collective-permute-start
  12.8 2.1 add_reduce_fusion.3
  15.1 5.1 %collective-permute-start.2 = (f32[2,384,128]{2,1,0:T(8,128)S(1)}, f32[2,384,128]{2,1,0:T(8,128)S(1)}, u32[]{:S(2)}, u32[]{:S(2)}) collective-permute-start(f32[2,384,128]{2,1,0:T(8,128)S(1)} %get-tuple-element.611), channel_id=1, source_target_pairs={{0,1},{2,3},{4,5},{6,7},{8,9},{10,11},{12,13},{14,15},{16,17},{18,... | collective-permute-start | bytes 1179656 | tf_op jit(solution)/shard_map/ppermute | solution.py:25
  21.6 5.7 %collective-permute-done.2 = f32[2,384,128]{2,1,0:T(8,128)S(1)} collective-permute-done((f32[2,384,128]{2,1,0:T(8,128)S(1)}, f32[2,384,128]{2,1,0:T(8,128)S(1)}, u32[]{:S(2)}, u32[]{:S(2)}) %collective-permute-start.2) | collective-permute-done | bytes 393248 | tf_op jit(solution)/shard_map/ppermute | solution.py:25
  27.4 4.7 %collective-permute-done.3 = f32[2,384,128]{2,1,0:T(8,128)S(1)} collective-permute-done((f32[2,384,128]{2,1,0:T(8,128)S(1)}, f32[2,384,128]{2,1,0:T(8,128)S(1)}, u32[]{:S(2)}, u32[]{:S(2)}) %collective-permute-start.3) | collective-permute-done | bytes 393248 | tf_op jit(solution)/shard_map/ppermute | solution.py:26
  33.4 1.7 broadcast_in_dim.23
  35.1 113.0 %while.34 = (s32[]{:T(128)}, f32[12,128,128]{2,1,0:T(8,128)}, f32[12,128,128]{2,1,0:T(8,128)}, f32[128,128]{1,0:T(8,128)}, f32[3,384,512]{2,1,0:T(8,128)}, /*ind...) while((s32[]{:T(128)}, f32[12,128,128]{2,1,0:T(8,128)}, ...), condition=%wide.region_6.7_spmd.clone, body=%wide.region_1.6_spmd.clone.sunk | while | flops 4844257280 | bytes 53870996 | solution.py:203
  40.6 1.7 fusion.160
  42.5 2.7 fusion.162
  45.4 2.8 convolution_bitcast_fusion.4
  48.6 2.8 fusion.164
  51.6 2.7 convolution_bitcast_fusion.5
  58.8 2.8 dynamic_update_slice.12
  67.1 1.8 fusion.160
  69.1 2.7 fusion.162
  72.0 2.8 convolution_bitcast_fusion.4
  75.2 2.8 fusion.164
  78.2 2.7 convolution_bitcast_fusion.5
  82.9 2.8 fusion.166
  86.9 2.8 dynamic_update_slice.12
  95.2 1.8 fusion.160
  97.2 2.7 fusion.162
  100.1 2.8 convolution_bitcast_fusion.4
  103.3 2.8 fusion.164
  106.3 2.7 convolution_bitcast_fusion.5
  111.0 2.8 fusion.166
  115.0 4.1 %dynamic_update_slice.12 = f32[3,384,512]{2,1,0:T(8,128)} dynamic-update-slice(f32[3,384,512]{2,1,0:T(8,128)} %get-tuple-element.770, f32[3,128,128]{2,1,0:T(8,128)S(1)} %maximum_add_fusion.2, s32[]{:T(128)} %constant.327.clone.1..sunk, s32[]{:T(128)S(6)} %select_n.67, s32[]{:T(128)S(6)} %select_n.68) | dynamic-update-slice | bytes 393220 | tf_op jit(solution)/shard_map/while/body/eval_jaxpr/dynamic_update_slice | solution.py:187
  124.6 1.8 fusion.160
  126.6 2.7 fusion.162
  129.4 2.8 convolution_bitcast_fusion.4
  132.7 2.8 fusion.164
  135.6 2.7 convolution_bitcast_fusion.5
  140.3 2.8 fusion.166
  144.3 3.8 %dynamic_update_slice.12 = f32[3,384,512]{2,1,0:T(8,128)} dynamic-update-slice(f32[3,384,512]{2,1,0:T(8,128)} %get-tuple-element.770, f32[3,128,128]{2,1,0:T(8,128)S(1)} %maximum_add_fusion.2, s32[]{:T(128)} %constant.327.clone.1..sunk, s32[]{:T(128)S(6)} %select_n.67, s32[]{:T(128)S(6)} %select_n.68) | dynamic-update-slice | bytes 393220 | tf_op jit(solution)/shard_map/while/body/eval_jaxpr/dynamic_update_slice | solution.py:187
  148.1 2.8 fusion.66
  151.0 4.1 %collective-permute-start.4 = (f32[3,128,512]{2,1,0:T(8,128)}, f32[3,128,512]{2,1,0:T(8,128)S(1)}, u32[]{:S(2)}, u32[]{:S(2)}) collective-permute-start(f32[3,128,512]{2,1,0:T(8,128)} %get-tuple-element.607), channel_id=1, source_target_pairs={{0,2},{2,4},{4,6},{6,8},{8,10},{10,12},{12,14},{14,16},{16,18},{18... | collective-permute-start | bytes 2359304 | tf_op jit(solution)/shard_map/ppermute | solution.py:25
  156.3 1.7 reduce_sum.93
  158.3 2.1 copy.40
  160.4 51.2 %all-reduce = (f32[]{:T(128)}, f32[]{:T(128)}) all-reduce(f32[]{:T(128)} %reduce_sum.93, f32[]{:T(128)} %get-tuple-element.473), channel_id=1, replica_groups=mesh['scan'=16,'tile'=2] {'scan','tile'}, use_global_device_ids=true, to_apply=%region_11.12 | all-reduce | flops 2 | bytes 16 | tf_op jit(solution)/shard_map/psum | solution.py:105
  212.9 2.1 constant_dynamic-update-slice_fusion.4
  218.9 6.4 %collective-permute-start.6 = (f32[3,640,128]{2,1,0:T(8,128)}, f32[3,640,128]{2,1,0:T(8,128)}, u32[]{:S(2)}, u32[]{:S(2)}) collective-permute-start(f32[3,640,128]{2,1,0:T(8,128)} %get-tuple-element.606), channel_id=1, source_target_pairs={{0,1},{2,3},{4,5},{6,7},{8,9},{10,11},{12,13},{14,15},{16,17},{18,... | collective-permute-start | bytes 2949128 | tf_op jit(solution)/shard_map/ppermute | solution.py:25
  226.5 71.0 %all-reduce.4.cloned.1.call-done = (f32[24,16384]{1,0:T(8,128)}, f32[1,16384]{1,0:T(1,128)}) async-done(((f32[24,16384]{1,0:T(8,128)}, f32[1,16384]{1,0:T(1,128)}), (f32[24,16384]{1,0:T(8,128)}, f32[1,16384]{1,0:T(1,128)})) %all-reduce.4.cloned.1.call-update) | async-done | bytes 1638416 | tf_op jit(solution)/shard_map/psum | solution.py:216
  298.5 3.5 %bitcast_add_fusion = f32[24,16384]{1,0:T(8,128)} fusion(f32[3,8,128,128]{3,2,1,0:T(8,128)S(1)} %bitcast.192, f32[24,16384]{1,0:T(8,128)} %get-tuple-element.588, f32[16384]{0:T(1024)S(1)} %bitcast.201), kind=kLoop, calls=%fused_computation.67 | loop fusion | flops 786432 | bytes 4784128 | tf_op jit(solution)/shard_map/add | solution.py:217
  302.0 5.7 %slice.446 = f32[12,16384]{1,0:T(8,128)S(1)} slice(f32[24,16384]{1,0:T(8,128)} %bitcast_add_fusion), slice={[1:24:2], [0:16384:1]} | slice | bytes 1572864 | tf_op jit(solution)/shard_map/slice | solution.py:79
  307.7 5.7 %slice.445 = f32[12,16384]{1,0:T(8,128)S(1)} slice(f32[24,16384]{1,0:T(8,128)} %bitcast_add_fusion), slice={[0:24:2], [0:16384:1]} | slice | bytes 1572864 | tf_op jit(solution)/shard_map/slice | solution.py:78
  324.4 2.0 fusion.56
  326.4 2.0 fusion.60
  329.1 2.3 convolution_subtract_fusion
  (162 shorter events, 57.1 us)
Async XLA Ops:
  7.2 7.8 %copy-start.10 = (f32[2,128,256]{2,1,0:T(8,128)S(1)}, f32[2,128,256]{2,1,0:T(8,128)}, u32[]{:S(2)}) copy-start(f32[2,128,256]{2,1,0:T(8,128)} %param.28) | copy-start | bytes 786436
  7.2 290.4 %all-reduce.4.cloned.1.call-start = ((), (), s32[]{:S(2)}) async-start(), calls=%async_computation | async-start | bytes 3276800 | tf_op jit(solution)/shard_map/psum | solution.py:216
  7.2 7.8 %collective-permute-start.1 = (f32[2,128,256]{2,1,0:T(8,128)}, f32[2,128,256]{2,1,0:T(8,128)S(1)}, u32[]{:S(2)}, u32[]{:S(2)}) collective-permute-start(f32[2,128,256]{2,1,0:T(8,128)} %param.28), channel_id=1, source_target_pairs={{2,0},{4,2},{6,4},{8,6},{10,8},{12,10},{14,12},{16,14},{18,16},{20... | collective-permute-start | bytes 786440 | tf_op jit(solution)/shard_map/ppermute | solution.py:26
  8.7 6.3 %collective-permute-start = (f32[2,128,256]{2,1,0:T(8,128)}, f32[2,128,256]{2,1,0:T(8,128)S(1)}, u32[]{:S(2)}, u32[]{:S(2)}) collective-permute-start(f32[2,128,256]{2,1,0:T(8,128)} %param.28), channel_id=1, source_target_pairs={{0,2},{2,4},{4,6},{6,8},{8,10},{10,12},{12,14},{14,16},{16,18},{18... | collective-permute-start | bytes 786440 | tf_op jit(solution)/shard_map/ppermute | solution.py:25
  15.0 6.5 %copy-start.2 = (f32[12,2,128,128]{3,2,1,0:T(8,128)S(1)}, f32[12,2,128,128]{3,2,1,0:T(8,128)}, u32[]{:S(2)}) copy-start(f32[12,2,128,128]{3,2,1,0:T(8,128)} %param.26) | copy-start | bytes 4718596
  15.1 12.2 %collective-permute-start.2 = (f32[2,384,128]{2,1,0:T(8,128)S(1)}, f32[2,384,128]{2,1,0:T(8,128)S(1)}, u32[]{:S(2)}, u32[]{:S(2)}) collective-permute-start(f32[2,384,128]{2,1,0:T(8,128)S(1)} %get-tuple-element.611), channel_id=1, source_target_pairs={{0,1},{2,3},{4,5},{6,7},{8,9},{10,11},{12,13},{14,15},{16,17},{18,... | collective-permute-start | bytes 1179656 | tf_op jit(solution)/shard_map/ppermute | solution.py:25
  20.2 11.9 %collective-permute-start.3 = (f32[2,384,128]{2,1,0:T(8,128)S(1)}, f32[2,384,128]{2,1,0:T(8,128)S(1)}, u32[]{:S(2)}, u32[]{:S(2)}) collective-permute-start(f32[2,384,128]{2,1,0:T(8,128)S(1)} %get-tuple-element.612), channel_id=1, source_target_pairs={{1,0},{3,2},{5,4},{7,6},{9,8},{11,10},{13,12},{15,14},{17,16},{19,... | collective-permute-start | bytes 1179656 | tf_op jit(solution)/shard_map/ppermute | solution.py:26
  56.2 1.4 copy-start.4
  56.3 1.4 copy-start.5
  82.8 2.8 copy-start.4
  82.9 2.8 copy-start.5
  111.0 2.8 copy-start.4
  111.0 2.8 copy-start.5
  140.3 2.8 copy-start.4
  140.3 2.8 copy-start.5
  148.1 9.9 %copy-start = (f32[12,128,128]{2,1,0:T(8,128)S(1)}, f32[12,128,128]{2,1,0:T(8,128)}, u32[]{:S(2)}) copy-start(f32[12,128,128]{2,1,0:T(8,128)} %get-tuple-element.471) | copy-start | bytes 2359300
  148.1 9.9 %copy-start.1 = (f32[12,128,128]{2,1,0:T(8,128)S(1)}, f32[12,128,128]{2,1,0:T(8,128)}, u32[]{:S(2)}) copy-start(f32[12,128,128]{2,1,0:T(8,128)} %get-tuple-element.470) | copy-start | bytes 2359300
  151.0 61.9 %collective-permute-start.4 = (f32[3,128,512]{2,1,0:T(8,128)}, f32[3,128,512]{2,1,0:T(8,128)S(1)}, u32[]{:S(2)}, u32[]{:S(2)}) collective-permute-start(f32[3,128,512]{2,1,0:T(8,128)} %get-tuple-element.607), channel_id=1, source_target_pairs={{0,2},{2,4},{4,6},{6,8},{8,10},{10,12},{12,14},{14,16},{16,18},{18... | collective-permute-start | bytes 2359304 | tf_op jit(solution)/shard_map/ppermute | solution.py:25
  155.0 60.0 %collective-permute-start.5 = (f32[3,128,512]{2,1,0:T(8,128)}, f32[3,128,512]{2,1,0:T(8,128)S(1)}, u32[]{:S(2)}, u32[]{:S(2)}) collective-permute-start(f32[3,128,512]{2,1,0:T(8,128)} %get-tuple-element.608), channel_id=1, source_target_pairs={{2,0},{4,2},{6,4},{8,6},{10,8},{12,10},{14,12},{16,14},{18,16},{20... | collective-permute-start | bytes 2359304 | tf_op jit(solution)/shard_map/ppermute | solution.py:26
  212.9 2.2 copy-start.7
  215.1 1.0 copy-start.9
  216.0 9.3 %copy-start.8 = (f32[3,128,512]{2,1,0:T(8,128)S(1)}, f32[3,128,512]{2,1,0:T(8,128)}, u32[]{:S(2)}) copy-start(f32[3,128,512]{2,1,0:T(8,128)} %copy-done.7) | copy-start | bytes 2359300
  217.5 81.0 %copy-start.3 = (f32[12,2,128,128]{3,2,1,0:T(8,128)S(1)}, f32[12,2,128,128]{3,2,1,0:T(8,128)}, u32[]{:S(2)}) copy-start(f32[12,2,128,128]{3,2,1,0:T(8,128)} %param.26) | copy-start | bytes 4718596
  217.5 118.0 %collective-permute-start.7 = (f32[3,640,128]{2,1,0:T(8,128)}, f32[3,640,128]{2,1,0:T(8,128)}, u32[]{:S(2)}, u32[]{:S(2)}) collective-permute-start(f32[3,640,128]{2,1,0:T(8,128)} %get-tuple-element.605), channel_id=1, source_target_pairs={{1,0},{3,2},{5,4},{7,6},{9,8},{11,10},{13,12},{15,14},{17,16},{19,... | collective-permute-start | bytes 2949128 | tf_op jit(solution)/shard_map/ppermute | solution.py:26
  218.9 115.6 %collective-permute-start.6 = (f32[3,640,128]{2,1,0:T(8,128)}, f32[3,640,128]{2,1,0:T(8,128)}, u32[]{:S(2)}, u32[]{:S(2)}) collective-permute-start(f32[3,640,128]{2,1,0:T(8,128)} %get-tuple-element.606), channel_id=1, source_target_pairs={{0,1},{2,3},{4,5},{6,7},{8,9},{10,11},{12,13},{14,15},{16,17},{18,... | collective-permute-start | bytes 2949128 | tf_op jit(solution)/shard_map/ppermute | solution.py:25
  329.1 2.4 copy-start.6
  335.4 5.0 %copy-start.11 = (f32[2,128,256]{2,1,0:T(8,128)S(1)}, f32[2,128,256]{2,1,0:T(8,128)}, u32[]{:S(2)}) copy-start(f32[2,128,256]{2,1,0:T(8,128)} %param.28) | copy-start | bytes 786436
Sparse Core Ops, SparseCore 0:
  160.5 137.0 all-reduce.3
where the time goes:
time: 350 us; the launch traced here: 348 us
  waiting for transfers between devices  81.5 us (23%)
  matrix products  60.6 us (17%)
  other arithmetic  51.5 us (15%)
  blocking collectives  51.2 us (15%)
  local copies, waits for them, and re-layouts  46.1 us (13%)
  starting transfers between devices  24.1 us (7%)
  between operations  16.5 us (5%)
  loops' own time  16.4 us (5%)
    psum x1, waiting for transfers between devices, body(): grad_total, light_total = lax.psum((grad_rows, light_row), ('scan', 'tile'))  71 us
    psum x1, blocking collectives, global_totals(): return lax.psum((measured, modeled), ('scan', 'tile'))  51.2 us
    dot_general x8, matrix products, complex_section(): jnp.einsum('wx,cmxy->cmwy', table, stacked, precision=highest, preferred_...  22 us
    dot_general x8, matrix products, complex_section(): jnp.einsum('cmxy,yw->cmxw', stacked, table, precision=highest, preferred_...  21.8 us
    ppermute x4, starting transfers between devices, extended_2(): before = lax.ppermute(last, axis, up)  18.6 us
    another operation x1, loops' own time, body(): lax.fori_loop(0, position_count, one_position, initial)  16.4 us
    dynamic_update_slice x4, local copies, waits for them, and re-layouts, one_position(): lax.dynamic_update_slice(frame_sum, previous + addition, (zero_index, row...  13.5 us
    sub x4, other arithmetic, one_position(): grad_im = grad_im + patch_re[None] * change_im - patch_im[None] * change_re  9.88 us
  transfers between devices with their start and end apart: 9, of which 3 were waited for; matrix products, arithmetic and copies ran while one was open for 14% of the time, Pallas kernels for 0%

commit v1 on v0

v1 whole, which is shorter than its diff:
```python
import math

import jax
import jax.numpy as jnp
import numpy as np
from jax import lax
from jax.experimental import pallas as pl
from jax.experimental.pallas import tpu as pltpu
from jax.sharding import PartitionSpec as P

NS_STEPS = 8


highest = lax.Precision.HIGHEST
light_floor = 0.05
object_reg = 0.5
probe_reg = 1.0
total_eps = 1e-06


def extended_2(array, sides, width):
    for axis, dim in sides:
        size, length = (lax.axis_size(axis), array.shape[dim])
        up = [(i, (i + 1) % size) for i in range(size - 1)]
        down = [(j, i) for i, j in up]
        last = lax.slice_in_dim(array, length - width, length, axis=dim)
        first = lax.slice_in_dim(array, 0, width, axis=dim)
        before = lax.ppermute(last, axis, up)
        after = lax.ppermute(first, axis, down)
        array = jnp.concatenate([before, array, after], axis=dim)
    return array


def dft_tables(detector):
    indices = np.arange(detector, dtype=np.int64)
    angles = -2.0 * np.pi / detector * (indices[:, None] * indices[None, :] % detector)
    table_re = np.cos(angles) / np.sqrt(detector)
    table_im = np.sin(angles) / np.sqrt(detector)
    right = np.block([[table_re, table_im], [-table_im, table_re]]).astype(np.float32)
    left = np.ascontiguousarray(right.T)
    parts = []
    for table in (right, left):
        high = table.astype(jnp.bfloat16)
        low = (table - high.astype(np.float32)).astype(jnp.bfloat16)
        parts.append((high, low))
    (rh, rl), (lh, ll) = parts
    return (
        np.concatenate([rh, rl, rh], axis=0),
        np.concatenate([lh, ll, lh], axis=1),
        np.concatenate([rh, rl, rh], axis=1),
        np.concatenate([lh, ll, lh], axis=0),
    )


def halves(value):
    high = value.astype(jnp.bfloat16)
    low = (value - high.astype(jnp.float32)).astype(jnp.bfloat16)
    return high, low


def scan_kernel(
    offs, probe, patterns, extended, right_f, left_f, left_b, right_b,
    grad, light, frame_out, total_out,
    ext, frame, deep, half, far, power,
    *, block_rows, block_cols,
):
    modes = probe.shape[0]
    det = probe.shape[-1]
    count = patterns.shape[0]
    col_blocks = extended.shape[2] // det
    f32 = jnp.float32
    row_base = lax.axis_index("scan") * block_rows - det
    col_base = lax.axis_index("tile") * block_cols - det
    lanes = lax.broadcasted_iota(jnp.int32, (det, det), 1)
    for c in range(2):
        for j in range(col_blocks):
            ext[c, j] = extended[c, :, j * det : (j + 1) * det]
        ext[c, col_blocks] = jnp.zeros_like(ext[c, col_blocks])
    frame[...] = jnp.zeros_like(frame)
    grad[...] = jnp.zeros_like(grad)
    light[...] = jnp.zeros_like(light)
    acc = jnp.zeros((det, det), f32)
    for k in range(modes):
        acc = acc + probe[k, 0] * probe[k, 0] + probe[k, 1] * probe[k, 1]
    power[...] = acc

    def one(p, total):
        row = offs[p, 0] - row_base
        col = offs[p, 1] - col_base
        block = col // det
        shift = col - block * det
        back = lax.rem(det - shift, det)
        rows = pl.ds(row, det)

        def patch_part(c):
            first = pltpu.roll(ext[c, block, rows, :], back, 1)
            second = pltpu.roll(ext[c, block + 1, rows, :], back, 1)
            return jnp.where(lanes < det - shift, first, second)

        patch_re = patch_part(0)
        patch_im = patch_part(1)
        patch_light = patch_re * patch_re + patch_im * patch_im
        light[...] = light[...] + patch_light
        total = total + patch_light * power[...]
        for k in range(modes):
            at = pl.ds(k * det, det)
            pr, pi = probe[k, 0], probe[k, 1]
            for c, value in enumerate((pr * patch_re - pi * patch_im, pr * patch_im + pi * patch_re)):
                high, low = halves(value)
                deep[at, pl.ds(c * det, det)] = high
                deep[at, pl.ds((2 + c) * det, det)] = high
                deep[at, pl.ds((4 + c) * det, det)] = low
        half[...] = jnp.dot(deep[...], right_f[...], preferred_element_type=f32)
        model = jnp.zeros((det, det), f32)
        for k in range(0, modes, 2):
            lo_at, hi_at = pl.ds(k * det, det), pl.ds((k + 1) * det, det)
            first, second = half[lo_at, :], half[hi_at, :]
            paired = jnp.concatenate(
                [
                    jnp.concatenate([first[:, :det], second[:, :det]], axis=1),
                    jnp.concatenate([first[:, det:], second[:, det:]], axis=1),
                ],
                axis=0,
            )
            high, low = halves(paired)
            stacked = jnp.concatenate([high, high, low], axis=0)
            out = jnp.dot(left_f[...], stacked, preferred_element_type=f32)
            far[:, pl.ds(k * det, 2 * det)] = out
            squares = out * out
            both = squares[:det] + squares[det:]
            model = model + both[:, :det] + both[:, det:]
        factor = jnp.sqrt(patterns[p]) / jnp.sqrt(jnp.maximum(model, light_floor)) - 1.0
        wide = jnp.concatenate([factor, factor], axis=1)
        wide = jnp.concatenate([wide, wide], axis=0)
        for k in range(0, modes, 2):
            high, low = halves(far[:, pl.ds(k * det, 2 * det)] * wide)
            stacked = jnp.concatenate([high, high, low], axis=0)
            out = jnp.dot(left_b[...], stacked, preferred_element_type=f32)
            high, low = halves(out)
            for m in range(2):
                at = pl.ds((k + m) * det, det)
                for c in range(2):
                    part_h = high[c * det : (c + 1) * det, m * det : (m + 1) * det]
                    part_l = low[c * det : (c + 1) * det, m * det : (m + 1) * det]
                    deep[at, pl.ds(c * det, det)] = part_h
                    deep[at, pl.ds((2 + c) * det, det)] = part_h
                    deep[at, pl.ds((4 + c) * det, det)] = part_l
        half[...] = jnp.dot(deep[...], right_b[...], preferred_element_type=f32)
        num_re = jnp.zeros((det, det), f32)
        num_im = jnp.zeros((det, det), f32)
        for k in range(modes):
            at = pl.ds(k * det, det)
            cr, ci = half[at, :det], half[at, det:]
            pr, pi = probe[k, 0], probe[k, 1]
            grad[0, k] = grad[0, k] + patch_re * cr + patch_im * ci
            grad[1, k] = grad[1, k] + patch_re * ci - patch_im * cr
            num_re = num_re + pr * cr + pi * ci
            num_im = num_im + pr * ci - pi * cr
        zero = jnp.zeros((det, det), f32)
        for c, value in enumerate((num_re, num_im, power[...])):
            turned = pltpu.roll(value, shift, 1)
            frame[c, block, rows, :] = frame[c, block, rows, :] + jnp.where(lanes >= shift, turned, zero)
            frame[c, block + 1, rows, :] = frame[c, block + 1, rows, :] + jnp.where(lanes < shift, turned, zero)
        return total

    total_out[...] = lax.fori_loop(0, count, one, jnp.zeros((det, det), f32))
    for c in range(3):
        for j in range(col_blocks):
            frame_out[c, :, j * det : (j + 1) * det] = frame[c, j]


def scan_positions(offsets, probe_modes, patterns, extended, block_rows, block_cols):
    modes, _, det, _ = probe_modes.shape
    f32 = jnp.float32
    ext_rows, ext_cols = extended.shape[1:]
    col_blocks = ext_cols // det
    vmem = pl.BlockSpec(memory_space=pltpu.VMEM)
    tables = [jnp.asarray(t) for t in dft_tables(det)]

    def kernel(*refs):
        scan_kernel(*refs, block_rows=block_rows, block_cols=block_cols)

    return pl.pallas_call(
        kernel,
        name="scan_positions",
        out_shape=(
            jax.ShapeDtypeStruct((2, modes, det, det), f32),
            jax.ShapeDtypeStruct((det, det), f32),
            jax.ShapeDtypeStruct((3, ext_rows, ext_cols), f32),
            jax.ShapeDtypeStruct((det, det), f32),
        ),
        in_specs=[pl.BlockSpec(memory_space=pltpu.SMEM)] + [vmem] * 7,
        out_specs=(vmem,) * 4,
        scratch_shapes=[
            pltpu.VMEM((2, col_blocks + 1, ext_rows, det), f32),
            pltpu.VMEM((3, col_blocks + 1, ext_rows, det), f32),
            pltpu.VMEM((modes * det, 6 * det), jnp.bfloat16),
            pltpu.VMEM((modes * det, 2 * det), f32),
            pltpu.VMEM((2 * det, modes * det), f32),
            pltpu.VMEM((det, det), f32),
        ],
        compiler_params=pltpu.CompilerParams(vmem_limit_bytes=48 * 1024 * 1024),
    )(offsets, probe_modes, patterns, extended, *tables)


def newton_steps(gram_re, gram_im):
    mode_count = gram_re.shape[0]
    upper = jnp.concatenate([gram_re, -gram_im], axis=1)
    lower = jnp.concatenate([gram_im, gram_re], axis=1)
    embedded = jnp.concatenate([upper, lower], axis=0)
    frobenius = jnp.sqrt(jnp.sum(embedded * embedded))
    identity = jnp.eye(2 * mode_count, dtype=jnp.float32)
    current = embedded / frobenius
    inverse = identity
    for repeat in range(NS_STEPS):
        factor = 1.5 * identity - 0.5 * jnp.dot(
            inverse, current, precision=highest, preferred_element_type=jnp.float32
        )
        current = jnp.dot(current, factor, precision=highest, preferred_element_type=jnp.float32)
        inverse = jnp.dot(factor, inverse, precision=highest, preferred_element_type=jnp.float32)
    inverse = inverse / jnp.sqrt(frobenius)
    return (inverse[:mode_count, :mode_count], inverse[mode_count:, :mode_count])


def gram_parts(mode_rows):
    real_rows = mode_rows[: mode_rows.shape[0] // 2]
    imag_rows = mode_rows[mode_rows.shape[0] // 2 :]
    gram_re = jnp.dot(
        real_rows, real_rows.T, precision=highest, preferred_element_type=jnp.float32
    ) + jnp.dot(imag_rows, imag_rows.T, precision=highest, preferred_element_type=jnp.float32)
    gram_im = jnp.dot(
        real_rows, imag_rows.T, precision=highest, preferred_element_type=jnp.float32
    ) - jnp.dot(imag_rows, real_rows.T, precision=highest, preferred_element_type=jnp.float32)
    return (gram_re, gram_im)


def orthonormal_rows(mode_rows, gram_re, gram_im, power_ratio):
    real_rows = mode_rows[: mode_rows.shape[0] // 2]
    imag_rows = mode_rows[mode_rows.shape[0] // 2 :]
    mix_re, mix_im = newton_steps(gram_re, gram_im)
    ortho_re = jnp.dot(
        mix_re.T, real_rows, precision=highest, preferred_element_type=jnp.float32
    ) - jnp.dot(mix_im.T, imag_rows, precision=highest, preferred_element_type=jnp.float32)
    ortho_im = jnp.dot(
        mix_im.T, real_rows, precision=highest, preferred_element_type=jnp.float32
    ) + jnp.dot(mix_re.T, imag_rows, precision=highest, preferred_element_type=jnp.float32)
    weight = jnp.sqrt(power_ratio * jnp.diagonal(gram_re))
    return jnp.stack([ortho_re, ortho_im], axis=1) * weight[:, None, None]


def fold_interior(frame_sum, folded, detector, block_rows, block_cols):
    rows_end = block_rows + 3 * detector
    cols_end = block_cols + 3 * detector
    centre_rows = slice(2 * detector, 2 * detector + block_rows)
    centre_cols = slice(2 * detector, 2 * detector + block_cols)
    interior = frame_sum[:, detector : detector + block_rows, detector : detector + block_cols]
    interior = interior.at[:, :detector, :].add(folded[:, :detector, centre_cols])
    interior = interior.at[:, block_rows - detector :, :].add(folded[:, rows_end:, centre_cols])
    interior = interior.at[:, :, :detector].add(folded[:, centre_rows, :detector])
    interior = interior.at[:, :, block_cols - detector :].add(folded[:, centre_rows, cols_end:])
    interior = interior.at[:, :detector, :detector].add(folded[:, :detector, :detector])
    interior = interior.at[:, :detector, block_cols - detector :].add(
        folded[:, :detector, cols_end:]
    )
    interior = interior.at[:, block_rows - detector :, :detector].add(
        folded[:, rows_end:, :detector]
    )
    interior = interior.at[:, block_rows - detector :, block_cols - detector :].add(
        folded[:, rows_end:, cols_end:]
    )
    return interior


def body(probe_modes, patterns, specimen, offsets):
    detector = probe_modes.shape[-1]
    mode_count = probe_modes.shape[0]
    block_rows = specimen.shape[1]
    block_cols = specimen.shape[2]
    extended = extended_2(specimen, (("scan", 1), ("tile", 2)), detector)
    grad, light_sum, frame_sum, model_grid = scan_positions(
        offsets, probe_modes, patterns, extended, block_rows, block_cols
    )
    pixels = detector * detector
    totals = jnp.stack([jnp.sum(patterns, axis=(0, 1)), jnp.sum(model_grid, axis=0)])
    packed = jnp.concatenate(
        [
            grad.reshape(2 * mode_count * detector, detector),
            light_sum,
            jnp.pad(totals, ((0, 6), (0, 0))),
        ],
        axis=0,
    )
    summed = lax.psum(packed, ("scan", "tile"))
    rows_grad = 2 * mode_count * detector
    grad_total = summed[:rows_grad].reshape(2 * mode_count, pixels)
    light_total = summed[rows_grad : rows_grad + detector].reshape(1, pixels)
    measured_all = jnp.sum(summed[rows_grad + detector])
    model_all = jnp.sum(summed[rows_grad + detector + 1])
    power_ratio = measured_all / (model_all + total_eps)
    folded = extended_2(frame_sum, (("scan", 1), ("tile", 2)), detector)
    interior = fold_interior(frame_sum, folded, detector, block_rows, block_cols)
    new_specimen = specimen + interior[0:2] / (interior[2] + object_reg)[None]
    probe_rows = jnp.swapaxes(probe_modes, 0, 1).reshape(2 * mode_count, pixels)
    updated = probe_rows + grad_total / (light_total + probe_reg)
    gram_re, gram_im = gram_parts(updated)
    new_probe = orthonormal_rows(updated, gram_re, gram_im, power_ratio).reshape(probe_modes.shape)
    return (new_probe, new_specimen)


def solution(mesh):
    return jax.shard_map(
        body,
        mesh=mesh,
        in_specs=(
            P(),
            P(("scan", "tile"), None, None),
            P(None, "scan", "tile"),
            P(("scan", "tile"), None),
        ),
        out_specs=(P(), P(None, "scan", "tile")),
        check_vma=False,
    )
```

time: 350 us -> 251 us (0.72)
  waiting for transfers between devices: 81.5 us -> 139 us
  blocking collectives: 51.2 us -> 0 us
  matrix products: 60.6 us -> 14.8 us
  other arithmetic: 51.5 us -> 16.9 us
  local copies, waits for them, and re-layouts: 46.1 us -> 18.1 us
  Pallas kernels: 0 us -> 21.6 us
  loops' own time: 16.4 us -> 0 us
    psum x1, waiting for transfers between devices: 71 us -> 125 us  [body(): summed = lax.psum(packed, ('scan', 'tile'))]
    psum x1 -> x0, blocking collectives: 51.2 us -> none  [global_totals(): return lax.psum((measured, modeled), ('scan', 'tile'))]
    dot_general x16 -> x0, matrix products: 43.8 us -> none  [the longest x8 22 us: complex_section(): jnp.einsum('wx,cmxy->cmwy', table, stacked, precision=highest, preferred_...]
    pallas_call x0 -> x1, Pallas kernels: none -> 21.6 us  [scan_positions(): pl.pallas_call(kernel, name='scan_positions', out_shape=(jax.ShapeDtypeSt...]
    another operation x1 -> x0, loops' own time: 16.4 us -> none  [body(): lax.fori_loop(0, position_count, one_position, initial)]
    dynamic_update_slice x4 -> x0, local copies, waits for them, and re-layouts: 13.5 us -> none  [one_position(): lax.dynamic_update_slice(frame_sum, previous + addition, (zero_index, row...]
    sub x17 -> x0, other arithmetic: 13 us -> none  [the longest x4 9.88 us: one_position(): grad_im = grad_im + patch_re[None] * change_im - patch_im[None] * change_re]
    add x9 -> x1, other arithmetic: 12.3 us -> 0.75 us  [body(): new_specimen = specimen + interior[0:2] / (interior[2] + object_reg)[None]]
  transfers between devices with their start and end apart: 9 -> 9, of which waited for: 3 -> 5; matrix products, arithmetic and copies ran while one was open for 14% -> 14% of each run, Pallas kernels for 0% -> 0%
where the time goes in v1:
time: 251 us
  waiting for transfers between devices  139 us (55%)
  starting transfers between devices  23.7 us (9%)
  Pallas kernels  21.6 us (9%)
  local copies, waits for them, and re-layouts  18.1 us (7%)
  other arithmetic  16.9 us (7%)
  between operations  16.3 us (6%)
  matrix products  14.8 us (6%)
    psum x1, waiting for transfers between devices, body(): summed = lax.psum(packed, ('scan', 'tile'))  125 us
    pallas_call x1, Pallas kernels, scan_positions(): pl.pallas_call(kernel, name='scan_positions', out_shape=(jax.ShapeDtypeSt...  21.6 us
    ppermute x4, starting transfers between devices, extended_2(): before = lax.ppermute(last, axis, up)  18.5 us
    ppermute x4, waiting for transfers between devices, extended_2(): after = lax.ppermute(first, axis, down)  9.78 us
    unnamed x29, local copies, waits for them, and re-layouts  6.78 us
    ppermute x4, starting transfers between devices, extended_2(): after = lax.ppermute(first, axis, down)  5.15 us
  transfers between devices with their start and end apart: 9, of which 5 were waited for; matrix products, arithmetic and copies ran while one was open for 14% of the time, Pallas kernels for 0%

profile of v1, /device:TPU:0, one launch (start us, length us, event | category | flops | bytes accessed | tf_op | source)
XLA Modules:
  0.0 250.5 jit_solution(18137112386487962874)
XLA Ops:
  7.2 2.4 collective-permute-start
  9.6 1.3 collective-permute-start.1
  11.0 1.0 constant_dynamic-update-slice_fusion.1
  12.0 3.4 %collective-permute-done.1 = f32[2,128,256]{2,1,0:T(8,128)S(1)} collective-permute-done((f32[2,128,256]{2,1,0:T(8,128)}, f32[2,128,256]{2,1,0:T(8,128)S(1)}, u32[]{:S(2)}, u32[]{:S(2)}) %collective-permute-start.1) | collective-permute-done | bytes 262176 | tf_op jit(solution)/shard_map/ppermute | solution.py:29
  15.4 0.9 fusion.39
  16.3 3.4 %collective-permute-start.2 = (f32[2,384,128]{2,1,0:T(8,128)}, f32[2,384,128]{2,1,0:T(8,128)S(1)}, u32[]{:S(2)}, u32[]{:S(2)}) collective-permute-start(f32[2,384,128]{2,1,0:T(8,128)} %get-tuple-element.128), channel_id=1, source_target_pairs={{0,1},{2,3},{4,5},{6,7},{8,9},{10,11},{12,13},{14,15},{16,17},{18,... | collective-permute-start | bytes 1179656 | tf_op jit(solution)/shard_map/ppermute | solution.py:28
  19.8 1.3 collective-permute-start.3
  21.2 4.6 %collective-permute-done.2 = f32[2,384,128]{2,1,0:T(8,128)S(1)} collective-permute-done((f32[2,384,128]{2,1,0:T(8,128)}, f32[2,384,128]{2,1,0:T(8,128)S(1)}, u32[]{:S(2)}, u32[]{:S(2)}) %collective-permute-start.2) | collective-permute-done | bytes 393248 | tf_op jit(solution)/shard_map/ppermute | solution.py:28
  25.7 4.6 %collective-permute-done.3 = f32[2,384,128]{2,1,0:T(8,128)S(1)} collective-permute-done((f32[2,384,128]{2,1,0:T(8,128)}, f32[2,384,128]{2,1,0:T(8,128)S(1)}, u32[]{:S(2)}, u32[]{:S(2)}) %collective-permute-start.3) | collective-permute-done | bytes 393248 | tf_op jit(solution)/shard_map/ppermute | solution.py:29
  30.3 1.3 pad_maximum_fusion.1.refs_3_
  31.7 1.0 copy-done.5
  32.7 21.6 %scan_positions.1 = (f32[2,12,128,128]{3,2,1,0:T(8,128)S(1)}, f32[128,128]{1,0:T(8,128)S(1)}, f32[3,384,512]{2,1,0:T(8,128)}, f32[128,128]{1,0:T(8,128)S(1)}) custom-call(s32[4,2]{1,0:T(4,128)S(1)} %copy.14.refs_0_, f32[12,2,128,128]{3,2,1,0:T(8,128)S(1)} %copy-done, f32[4,128,128]{2,1,0:T(8,128)S(1)} %copy-done.1, ...), custom_call_target="tpu_custom_call" | custom-call | tf_op jit(solution)/shard_map/scan_positions/pallas_call | solution.py:183
  54.3 2.8 %fusion.38 = (f32[3,128,512]{2,1,0:T(8,128)}, f32[3,128,512]{2,1,0:T(8,128)}) fusion(f32[3,384,512]{2,1,0:T(8,128)} %get-tuple-element.121), kind=kLoop, calls=%fused_computation.85 | loop fusion | bytes 3145728 | tf_op jit(solution)/shard_map/slice | solution.py:26
  57.0 6.1 %collective-permute-start.4 = (f32[3,128,512]{2,1,0:T(8,128)}, f32[3,128,512]{2,1,0:T(8,128)}, u32[]{:S(2)}, u32[]{:S(2)}) collective-permute-start(f32[3,128,512]{2,1,0:T(8,128)} %get-tuple-element.126), channel_id=1, source_target_pairs={{0,2},{2,4},{4,6},{6,8},{8,10},{10,12},{12,14},{14,16},{16,18},{18... | collective-permute-start | bytes 2359304 | tf_op jit(solution)/shard_map/ppermute | solution.py:28
  63.2 1.2 copy.13
  64.5 1.3 collective-permute-start.5
  65.8 1.3 pad_maximum_fusion
  67.2 1.3 constant_dynamic-update-slice_fusion.5
  69.2 1.8 collective-permute-done.5
  71.1 1.5 fusion.37
  72.6 1.3 collective-permute-start.7
  73.9 6.5 %collective-permute-start.6 = (f32[3,640,128]{2,1,0:T(8,128)}, f32[3,640,128]{2,1,0:T(8,128)}, u32[]{:S(2)}, u32[]{:S(2)}) collective-permute-start(f32[3,640,128]{2,1,0:T(8,128)} %get-tuple-element.125), channel_id=1, source_target_pairs={{0,1},{2,3},{4,5},{6,7},{8,9},{10,11},{12,13},{14,15},{16,17},{18,... | collective-permute-start | bytes 2949128 | tf_op jit(solution)/shard_map/ppermute | solution.py:28
  80.4 1.2 slice_add_fusion
  81.6 124.7 %all-reduce.3.cloned.1.call-done = f32[3208,128]{1,0:T(8,128)} async-done(((f32[3208,128]{1,0:T(8,128)}), f32[3208,128]{1,0:T(8,128)}) %all-reduce.3.cloned.1.call-update) | async-done | bytes 1642512 | tf_op jit(solution)/shard_map/psum | solution.py:293
  206.3 1.4 slice-done
  207.7 1.4 reshape.270
  209.2 0.8 fusion.30
  210.0 2.8 %bitcast_add_fusion = f32[24,16384]{1,0:T(8,128)S(1)} fusion(f32[3,8,128,128]{3,2,1,0:T(8,128)} %bitcast.74, f32[24,16384]{1,0:T(8,128)} %reshape.270, f32[16384]{0:T(1024)S(1)} %fusion.30), kind=kLoop, calls=%fused_computation.4 | loop fusion | flops 786432 | bytes 4784128 | tf_op jit(solution)/shard_map/add | solution.py:304
  212.9 1.4 fusion.11
  214.3 1.5 fusion.20
  215.8 1.6 convolution_add_fusion.1
  217.4 1.5 fusion.40
  218.9 0.7 multiply_reduce_fusion
  224.0 1.1 fusion.14
  225.1 1.0 fusion.16
  226.1 1.0 convolution_add_fusion
  227.2 2.0 convolution_subtract_fusion
  229.9 1.2 copy.19
  231.3 1.2 copy-done.7
  234.4 1.3 bitcast_bitcast_fusion
  235.6 1.4 maximum_multiply_fusion
  237.0 1.0 fusion.28
  238.0 1.0 fusion.27
  239.0 1.0 fusion.26
  240.0 1.0 fusion.25
  241.0 1.0 fusion.24
  241.9 1.0 fusion.23
  243.0 0.7 fusion.22
  (64 shorter events, 6.3 us)
Async XLA Ops:
  7.2 13.9 %copy-start.10 = (s32[4,2]{0,1:T(2,128)S(1)}, s32[4,2]{0,1:T(2,128)}, u32[]{:S(2)}) copy-start(s32[4,2]{0,1:T(2,128)} %param.31) | copy-start | bytes 100
  7.2 199.1 %all-reduce.3.cloned.1.call-start = ((), (), s32[]{:S(2)}) async-start(), calls=%async_computation | async-start | bytes 3284992 | tf_op jit(solution)/shard_map/psum | solution.py:293
  7.2 3.8 %collective-permute-start = (f32[2,128,256]{2,1,0:T(8,128)}, f32[2,128,256]{2,1,0:T(8,128)S(1)}, u32[]{:S(2)}, u32[]{:S(2)}) collective-permute-start(f32[2,128,256]{2,1,0:T(8,128)} %param.30), channel_id=1, source_target_pairs={{0,2},{2,4},{4,6},{6,8},{8,10},{10,12},{12,14},{14,16},{16,18},{18... | collective-permute-start | bytes 786440 | tf_op jit(solution)/shard_map/ppermute | solution.py:28
  9.6 5.7 %collective-permute-start.1 = (f32[2,128,256]{2,1,0:T(8,128)}, f32[2,128,256]{2,1,0:T(8,128)S(1)}, u32[]{:S(2)}, u32[]{:S(2)}) collective-permute-start(f32[2,128,256]{2,1,0:T(8,128)} %param.30), channel_id=1, source_target_pairs={{2,0},{4,2},{6,4},{8,6},{10,8},{12,10},{14,12},{16,14},{18,16},{20... | collective-permute-start | bytes 786440 | tf_op jit(solution)/shard_map/ppermute | solution.py:29
  16.3 9.4 %collective-permute-start.2 = (f32[2,384,128]{2,1,0:T(8,128)}, f32[2,384,128]{2,1,0:T(8,128)S(1)}, u32[]{:S(2)}, u32[]{:S(2)}) collective-permute-start(f32[2,384,128]{2,1,0:T(8,128)} %get-tuple-element.128), channel_id=1, source_target_pairs={{0,1},{2,3},{4,5},{6,7},{8,9},{10,11},{12,13},{14,15},{16,17},{18,... | collective-permute-start | bytes 1179656 | tf_op jit(solution)/shard_map/ppermute | solution.py:28
  19.8 10.6 %collective-permute-start.3 = (f32[2,384,128]{2,1,0:T(8,128)}, f32[2,384,128]{2,1,0:T(8,128)S(1)}, u32[]{:S(2)}, u32[]{:S(2)}) collective-permute-start(f32[2,384,128]{2,1,0:T(8,128)} %get-tuple-element.129), channel_id=1, source_target_pairs={{1,0},{3,2},{5,4},{7,6},{9,8},{11,10},{13,12},{15,14},{17,16},{19,... | collective-permute-start | bytes 1179656 | tf_op jit(solution)/shard_map/ppermute | solution.py:29
  21.2 10.5 %copy-start = (f32[12,2,128,128]{3,2,1,0:T(8,128)S(1)}, f32[12,2,128,128]{3,2,1,0:T(8,128)}, u32[]{:S(2)}) copy-start(f32[12,2,128,128]{3,2,1,0:T(8,128)} %refs_1_.1) | copy-start | bytes 4718596
  21.2 10.5 %copy-start.1 = (f32[4,128,128]{2,1,0:T(8,128)S(1)}, f32[4,128,128]{2,1,0:T(8,128)}, u32[]{:S(2)}) copy-start(f32[4,128,128]{2,1,0:T(8,128)} %refs_2_.1) | copy-start | bytes 786436
  21.2 10.5 %copy-start.2 = (bf16[768,256]{1,0:T(8,128)(2,1)S(1)}, bf16[768,256]{1,0:T(8,128)(2,1)}, u32[]{:S(2)}) copy-start(bf16[768,256]{1,0:T(8,128)(2,1)} %constant.231.clone.refs_7_) | copy-start | bytes 1179652
  21.2 10.5 %copy-start.3 = (bf16[256,768]{1,0:T(8,128)(2,1)S(1)}, bf16[256,768]{1,0:T(8,128)(2,1)}, u32[]{:S(2)}) copy-start(bf16[256,768]{1,0:T(8,128)(2,1)} %constant.230.clone.refs_6_) | copy-start | bytes 1179652
  21.2 10.5 %copy-start.4 = (bf16[256,768]{1,0:T(8,128)(2,1)S(1)}, bf16[256,768]{1,0:T(8,128)(2,1)}, u32[]{:S(2)}) copy-start(bf16[256,768]{1,0:T(8,128)(2,1)} %constant.229.clone.refs_5_) | copy-start | bytes 1179652
  31.7 1.0 copy-start.5
  57.0 10.1 %collective-permute-start.4 = (f32[3,128,512]{2,1,0:T(8,128)}, f32[3,128,512]{2,1,0:T(8,128)}, u32[]{:S(2)}, u32[]{:S(2)}) collective-permute-start(f32[3,128,512]{2,1,0:T(8,128)} %get-tuple-element.126), channel_id=1, source_target_pairs={{0,2},{2,4},{4,6},{6,8},{8,10},{10,12},{12,14},{14,16},{16,18},{18... | collective-permute-start | bytes 2359304 | tf_op jit(solution)/shard_map/ppermute | solution.py:28
  64.5 6.5 %collective-permute-start.5 = (f32[3,128,512]{2,1,0:T(8,128)}, f32[3,128,512]{2,1,0:T(8,128)S(1)}, u32[]{:S(2)}, u32[]{:S(2)}) collective-permute-start(f32[3,128,512]{2,1,0:T(8,128)} %get-tuple-element.127), channel_id=1, source_target_pairs={{2,0},{4,2},{6,4},{8,6},{10,8},{12,10},{14,12},{16,14},{18,16},{20... | collective-permute-start | bytes 2359304 | tf_op jit(solution)/shard_map/ppermute | solution.py:29
  67.1 1.9 copy-start.6
  72.6 165.4 %collective-permute-start.7 = (f32[3,640,128]{2,1,0:T(8,128)}, f32[3,640,128]{2,1,0:T(8,128)}, u32[]{:S(2)}, u32[]{:S(2)}) collective-permute-start(f32[3,640,128]{2,1,0:T(8,128)} %get-tuple-element.124), channel_id=1, source_target_pairs={{1,0},{3,2},{5,4},{7,6},{9,8},{11,10},{13,12},{15,14},{17,16},{19,... | collective-permute-start | bytes 2949128 | tf_op jit(solution)/shard_map/ppermute | solution.py:29
  73.9 163.1 %collective-permute-start.6 = (f32[3,640,128]{2,1,0:T(8,128)}, f32[3,640,128]{2,1,0:T(8,128)}, u32[]{:S(2)}, u32[]{:S(2)}) collective-permute-start(f32[3,640,128]{2,1,0:T(8,128)} %get-tuple-element.125), channel_id=1, source_target_pairs={{0,1},{2,3},{4,5},{6,7},{8,9},{10,11},{12,13},{14,15},{16,17},{18,... | collective-permute-start | bytes 2949128 | tf_op jit(solution)/shard_map/ppermute | solution.py:28
  206.3 1.4 slice-start
  229.2 1.9 copy-start.8
  231.1 1.4 copy-start.7
  238.0 5.0 %copy-start.9 = (f32[2,128,256]{2,1,0:T(8,128)S(1)}, f32[2,128,256]{2,1,0:T(8,128)}, u32[]{:S(2)}) copy-start(f32[2,128,256]{2,1,0:T(8,128)} %param.30) | copy-start | bytes 786436
Sparse Core Ops, SparseCore 0:
  67.3 139.0 all-reduce.2

commit v2 on v1

--- a/solution.py
+++ b/solution.py
@@ -60,8 +60,8 @@
 
 def scan_kernel(
     offs, probe, patterns, extended, right_f, left_f, left_b, right_b,
-    grad, light, frame_out, total_out,
-    ext, frame, deep, half, far, power,
+    packed, frame_out,
+    ext, frame, deep, half, far, power, grad, light,
     *, block_rows, block_cols,
 ):
     modes = probe.shape[0]
@@ -163,7 +163,19 @@
             frame[c, block + 1, rows, :] = frame[c, block + 1, rows, :] + jnp.where(lanes < shift, turned, zero)
         return total
 
-    total_out[...] = lax.fori_loop(0, count, one, jnp.zeros((det, det), f32))
+    model_grid = lax.fori_loop(0, count, one, jnp.zeros((det, det), f32))
+    measured = jnp.zeros((det, det), f32)
+    for p in range(count):
+        measured = measured + patterns[p]
+    tiles = det // 8
+    for k in range(2 * modes):
+        packed[k * tiles : (k + 1) * tiles] = grad[k // modes, k % modes].reshape(tiles, 8, det)
+    last = 2 * modes * tiles
+    packed[last : last + tiles] = light[...].reshape(tiles, 8, det)
+    packed[last + tiles] = jnp.sum(measured.reshape(tiles, 8, det), axis=0)
+    packed[last + tiles + 1] = jnp.sum(model_grid.reshape(tiles, 8, det), axis=0)
+    for extra in range(last + tiles + 2, packed.shape[0]):
+        packed[extra] = jnp.zeros((8, det), f32)
     for c in range(3):
         for j in range(col_blocks):
             frame_out[c, :, j * det : (j + 1) * det] = frame[c, j]
@@ -184,19 +196,19 @@
         kernel,
         name="scan_positions",
         out_shape=(
-            jax.ShapeDtypeStruct((2, modes, det, det), f32),
-            jax.ShapeDtypeStruct((det, det), f32),
+            jax.ShapeDtypeStruct((packed_tiles(modes, det), 8, det), f32),
             jax.ShapeDtypeStruct((3, ext_rows, ext_cols), f32),
-            jax.ShapeDtypeStruct((det, det), f32),
         ),
         in_specs=[pl.BlockSpec(memory_space=pltpu.SMEM)] + [vmem] * 7,
-        out_specs=(vmem,) * 4,
+        out_specs=(vmem,) * 2,
         scratch_shapes=[
             pltpu.VMEM((2, col_blocks + 1, ext_rows, det), f32),
             pltpu.VMEM((3, col_blocks + 1, ext_rows, det), f32),
             pltpu.VMEM((modes * det, 6 * det), jnp.bfloat16),
             pltpu.VMEM((modes * det, 2 * det), f32),
             pltpu.VMEM((2 * det, modes * det), f32),
+            pltpu.VMEM((det, det), f32),
+            pltpu.VMEM((2, modes, det, det), f32),
             pltpu.VMEM((det, det), f32),
         ],
         compiler_params=pltpu.CompilerParams(vmem_limit_bytes=48 * 1024 * 1024),
@@ -248,27 +260,184 @@
     return jnp.stack([ortho_re, ortho_im], axis=1) * weight[:, None, None]
 
 
-def fold_interior(frame_sum, folded, detector, block_rows, block_cols):
-    rows_end = block_rows + 3 * detector
-    cols_end = block_cols + 3 * detector
-    centre_rows = slice(2 * detector, 2 * detector + block_rows)
-    centre_cols = slice(2 * detector, 2 * detector + block_cols)
-    interior = frame_sum[:, detector : detector + block_rows, detector : detector + block_cols]
-    interior = interior.at[:, :detector, :].add(folded[:, :detector, centre_cols])
-    interior = interior.at[:, block_rows - detector :, :].add(folded[:, rows_end:, centre_cols])
-    interior = interior.at[:, :, :detector].add(folded[:, centre_rows, :detector])
-    interior = interior.at[:, :, block_cols - detector :].add(folded[:, centre_rows, cols_end:])
-    interior = interior.at[:, :detector, :detector].add(folded[:, :detector, :detector])
-    interior = interior.at[:, :detector, block_cols - detector :].add(
-        folded[:, :detector, cols_end:]
-    )
-    interior = interior.at[:, block_rows - detector :, :detector].add(
-        folded[:, rows_end:, :detector]
-    )
-    interior = interior.at[:, block_rows - detector :, block_cols - detector :].add(
-        folded[:, rows_end:, cols_end:]
-    )
-    return interior
+fast_bits = (("scan", 1), ("scan", 2), ("scan", 4), ("tile", 1))
+halvings = 3
+
+
+def packed_tiles(modes, det):
+    tiles = (2 * modes + 1) * (det // 8) + 2
+    step = len(fast_bits) * 2**halvings
+    return -(-tiles // step) * step
+
+
+def mesh_bits():
+    bits = list(fast_bits)
+    for axis in ("scan", "tile"):
+        bit = 1
+        while bit < lax.axis_size(axis):
+            if (axis, bit) not in bits:
+                bits.append((axis, bit))
+            bit *= 2
+    return bits
+
+
+def directions():
+    return [(i, j) for i, j in ((1, 0), (-1, 0), (0, 1), (0, -1), (1, 1), (1, -1), (-1, 1), (-1, -1))]
+
+
+def exchange_kernel(bits, packed, frame, out, interior, acc, landing, *rest):
+    slots = rest[:8]
+    send_sem, recv_sem, fold_send, fold_recv = rest[8:]
+    pieces = len(fast_bits)
+    piece = packed.shape[0] // pieces
+    det = (frame.shape[1] - interior.shape[1]) // 2
+    block_rows, block_cols = interior.shape[1:]
+    here = {axis: lax.axis_index(axis) for axis in ("scan", "tile")}
+    sizes = {axis: lax.axis_size(axis) for axis in ("scan", "tile")}
+
+    def digit(axis, bit):
+        return (here[axis] // bit) % 2
+
+    def partner(axis, bit):
+        return {axis: here[axis] + bit * (1 - 2 * digit(axis, bit))}
+
+    def copy(src, dst, g, step, axis, bit):
+        return pltpu.make_async_remote_copy(
+            src_ref=src, dst_ref=dst, send_sem=send_sem.at[g, step], recv_sem=recv_sem.at[g, step],
+            device_id=partner(axis, bit), device_id_type=pl.DeviceIdType.MESH,
+        )
+
+    plans = []
+    for g in range(pieces):
+        order = [fast_bits[(g + i) % pieces] for i in range(pieces)] + bits[pieces:]
+        steps = []
+        start, size, land = g * piece, piece, 0
+        for axis, bit in order[:halvings]:
+            size //= 2
+            mine = digit(axis, bit)
+            keep, give = start + mine * size, start + (1 - mine) * size
+            steps.append(("halve", axis, bit, give, keep, size, land))
+            start = keep
+            land += size
+        for axis, bit in order[halvings:]:
+            steps.append(("both", axis, bit, start, start, size, land))
+            land += size
+        for axis, bit in reversed(order[:halvings]):
+            low = start - digit(axis, bit) * size
+            steps.append(("gather", axis, bit, start, low + (1 - digit(axis, bit)) * size, size, land))
+            start = low
+            land += size
+            size *= 2
+        plans.append(steps)
+    total = len(plans[0])
+
+    def make(g, step):
+        kind, axis, bit, give, keep, size, land = plans[g][step]
+        source = packed if step == 0 else acc
+        src = source.at[pl.ds(give, size)]
+        return copy(src, landing.at[g, pl.ds(land, size)], g, step, axis, bit)
+
+    def settle(g, step):
+        kind, axis, bit, give, keep, size, land = plans[g][step]
+        source = packed if step == 0 else acc
+        arrived = landing[g, pl.ds(land, size)]
+        acc[pl.ds(keep, size)] = arrived if kind == "gather" else source[pl.ds(keep, size)] + arrived
+
+    def span(shift, block):
+        low = {-1: 0, 0: det, 1: det + block}[shift]
+        return pl.ds(low, block if shift == 0 else det)
+
+    def inner(shift, block):
+        low = {-1: block - det, 0: 0, 1: 0}[shift]
+        return pl.ds(low, block if shift == 0 else det)
+
+    def valid(shift_rows, shift_cols):
+        row, col = here["scan"] + shift_rows, here["tile"] + shift_cols
+        return (row >= 0) & (row < sizes["scan"]) & (col >= 0) & (col < sizes["tile"])
+
+    def fold(index):
+        shift_rows, shift_cols = directions()[index]
+        return pltpu.make_async_remote_copy(
+            src_ref=frame.at[:, span(shift_rows, block_rows), span(shift_cols, block_cols)],
+            dst_ref=slots[index],
+            send_sem=fold_send.at[index],
+            recv_sem=fold_recv.at[index],
+            device_id={
+                "scan": (here["scan"] + shift_rows + sizes["scan"]) % sizes["scan"],
+                "tile": (here["tile"] + shift_cols + sizes["tile"]) % sizes["tile"],
+            },
+            device_id_type=pl.DeviceIdType.MESH,
+        )
+
+    def fold_start(indices):
+        for index in indices:
+            @pl.when(valid(*directions()[index]))
+            def _():
+                fold(index).start()
+
+    interior[...] = frame[:, det : det + block_rows, det : det + block_cols]
+    for g in range(pieces):
+        make(g, 0).start()
+    fold_start((0, 1))
+    for step in range(total):
+        for g in range(pieces):
+            make(g, step).wait()
+            settle(g, step)
+            if step + 1 < total:
+                make(g, step + 1).start()
+        if step == 0:
+            fold_start((2, 3))
+        if step == 1:
+            fold_start((4, 5, 6, 7))
+    out[...] = acc[...]
+    for index, (shift_rows, shift_cols) in enumerate(directions()):
+        @pl.when(valid(shift_rows, shift_cols))
+        def _():
+            fold(index).wait_send()
+
+        @pl.when(valid(-shift_rows, -shift_cols))
+        def _():
+            fold(index).wait_recv()
+            rows, cols = inner(shift_rows, block_rows), inner(shift_cols, block_cols)
+            interior[:, rows, cols] = interior[:, rows, cols] + slots[index][...]
+
+
+def exchange(packed, frame, det, block_rows, block_cols):
+    f32 = jnp.float32
+    bits = mesh_bits()
+    pieces = len(fast_bits)
+    piece = packed.shape[0] // pieces
+    steps = len(bits) + halvings
+    small = piece // 2**halvings
+    land = 2 * (piece - small) + (len(bits) - halvings) * small
+    vmem = pl.BlockSpec(memory_space=pltpu.VMEM)
+    slots = [
+        pltpu.VMEM((3, det if i else block_rows, det if j else block_cols), f32) for i, j in directions()
+    ]
+
+    def kernel(*refs):
+        exchange_kernel(bits, *refs)
+
+    return pl.pallas_call(
+        kernel,
+        name="exchange",
+        out_shape=(
+            jax.ShapeDtypeStruct(packed.shape, f32),
+            jax.ShapeDtypeStruct((3, block_rows, block_cols), f32),
+        ),
+        in_specs=[vmem, vmem],
+        out_specs=(vmem, vmem),
+        scratch_shapes=[
+            pltpu.VMEM(packed.shape, f32),
+            pltpu.VMEM((pieces, land) + packed.shape[1:], f32),
+            *slots,
+            pltpu.SemaphoreType.DMA((pieces, steps)),
+            pltpu.SemaphoreType.DMA((pieces, steps)),
+            pltpu.SemaphoreType.DMA((8,)),
+            pltpu.SemaphoreType.DMA((8,)),
+        ],
+        compiler_params=pltpu.CompilerParams(has_side_effects=True, vmem_limit_bytes=40 * 1024 * 1024),
+    )(packed, frame)
 
 
 def body(probe_modes, patterns, specimen, offsets):
@@ -277,28 +446,18 @@
     block_rows = specimen.shape[1]
     block_cols = specimen.shape[2]
     extended = extended_2(specimen, (("scan", 1), ("tile", 2)), detector)
-    grad, light_sum, frame_sum, model_grid = scan_positions(
+    packed, frame_sum = scan_positions(
         offsets, probe_modes, patterns, extended, block_rows, block_cols
     )
+    summed, interior = exchange(packed, frame_sum, detector, block_rows, block_cols)
     pixels = detector * detector
-    totals = jnp.stack([jnp.sum(patterns, axis=(0, 1)), jnp.sum(model_grid, axis=0)])
-    packed = jnp.concatenate(
-        [
-            grad.reshape(2 * mode_count * detector, detector),
-            light_sum,
-            jnp.pad(totals, ((0, 6), (0, 0))),
-        ],
-        axis=0,
-    )
-    summed = lax.psum(packed, ("scan", "tile"))
-    rows_grad = 2 * mode_count * detector
-    grad_total = summed[:rows_grad].reshape(2 * mode_count, pixels)
-    light_total = summed[rows_grad : rows_grad + detector].reshape(1, pixels)
-    measured_all = jnp.sum(summed[rows_grad + detector])
-    model_all = jnp.sum(summed[rows_grad + detector + 1])
+    tiles = detector // 8
+    last = 2 * mode_count * tiles
+    grad_total = summed[:last].reshape(2 * mode_count, pixels)
+    light_total = summed[last : last + tiles].reshape(1, pixels)
+    measured_all = jnp.sum(summed[last + tiles])
+    model_all = jnp.sum(summed[last + tiles + 1])
     power_ratio = measured_all / (model_all + total_eps)
-    folded = extended_2(frame_sum, (("scan", 1), ("tile", 2)), detector)
-    interior = fold_interior(frame_sum, folded, detector, block_rows, block_cols)
     new_specimen = specimen + interior[0:2] / (interior[2] + object_reg)[None]
     probe_rows = jnp.swapaxes(probe_modes, 0, 1).reshape(2 * mode_count, pixels)
     updated = probe_rows + grad_total / (light_total + probe_reg)

time: 251 us -> 144 us (0.57)
  waiting for transfers between devices: 139 us -> 12.5 us
  Pallas kernels: 21.6 us -> 84.7 us
  starting transfers between devices: 23.7 us -> 9.31 us
  between operations: 16.3 us -> 3.03 us
  other arithmetic: 16.9 us -> 7.8 us
  local copies, waits for them, and re-layouts: 18.1 us -> 9.9 us
    psum x1 -> x0, waiting for transfers between devices: 125 us -> none  [body(): summed = lax.psum(packed, ('scan', 'tile'))]
    pallas_call x0 -> x1, Pallas kernels: none -> 63.6 us  [exchange(): pl.pallas_call(kernel, name='exchange', out_shape=(jax.ShapeDtypeStruct(p...]
    ppermute x4 -> x2, starting transfers between devices: 18.5 us -> 6.73 us  [extended_2(): before = lax.ppermute(last, axis, up)]
    scatter-add x6 -> x0, other arithmetic: 5.9 us -> none  [the longest x1 1.02 us: fold_interior(): interior.at[:, :, block_cols - detector:]]
    slice x3 -> x1, local copies, waits for them, and re-layouts: 2.89 us -> 0.1 us  [body(): grad_total = summed[:last].reshape(2 * mode_count, pixels)]
    slice x2 -> x1, local copies, waits for them, and re-layouts: 3.67 us -> 1.02 us  [extended_2(): last = lax.slice_in_dim(array, length - width, length, axis=dim)]
    ppermute x4 -> x2, starting transfers between devices: 5.15 us -> 2.57 us  [extended_2(): after = lax.ppermute(first, axis, down)]
    ppermute x4 -> x2, waiting for transfers between devices: 9.78 us -> 8.82 us  [extended_2(): after = lax.ppermute(first, axis, down)]
  transfers between devices with their start and end apart: 9 -> 4, of which waited for: 5 -> 3; matrix products, arithmetic and copies ran while one was open for 14% -> 1% of each run, Pallas kernels for 0% -> 0%
where the time goes in v2:
time: 144 us; the launch traced here: 143 us
  Pallas kernels  84.7 us (59%)
  matrix products  16.1 us (11%)
  waiting for transfers between devices  12.5 us (9%)
  local copies, waits for them, and re-layouts  9.9 us (7%)
  starting transfers between devices  9.31 us (6%)
  other arithmetic  7.8 us (5%)
  between operations  3.03 us (2%)
    pallas_call x1, Pallas kernels, exchange(): pl.pallas_call(kernel, name='exchange', out_shape=(jax.ShapeDtypeStruct(p...  63.6 us
    pallas_call x1, Pallas kernels, scan_positions(): pl.pallas_call(kernel, name='scan_positions', out_shape=(jax.ShapeDtypeSt...  21.1 us
    ppermute x2, waiting for transfers between devices, extended_2(): after = lax.ppermute(first, axis, down)  8.82 us
    ppermute x2, starting transfers between devices, extended_2(): before = lax.ppermute(last, axis, up)  6.73 us
    unnamed x31, local copies, waits for them, and re-layouts  6.34 us
    ppermute x2, waiting for transfers between devices, extended_2(): before = lax.ppermute(last, axis, up)  3.66 us
    add x2, other arithmetic, body(): updated = probe_rows + grad_total / (light_total + probe_reg)  3.01 us
  transfers between devices with their start and end apart: 4, of which 3 were waited for; matrix products, arithmetic and copies ran while one was open for 1% of the time, Pallas kernels for 0%

profile of v2, /device:TPU:0, one launch (start us, length us, event | category | flops | bytes accessed | tf_op | source)
XLA Modules:
  0.0 143.2 jit_solution(11290893586453908665)
XLA Ops:
  0.6 2.5 %collective-permute-start = (f32[2,128,256]{2,1,0:T(8,128)}, f32[2,128,256]{2,1,0:T(8,128)S(1)}, u32[]{:S(2)}, u32[]{:S(2)}) collective-permute-start(f32[2,128,256]{2,1,0:T(8,128)} %param.10), channel_id=1, source_target_pairs={{0,2},{2,4},{4,6},{6,8},{8,10},{10,12},{12,14},{14,16},{16,18},{18... | collective-permute-start | bytes 786440 | tf_op jit(solution)/shard_map/ppermute | solution.py:28
  3.2 1.3 collective-permute-start.1
  4.6 1.0 constant_dynamic-update-slice_fusion.1
  5.5 3.4 %collective-permute-done.1 = f32[2,128,256]{2,1,0:T(8,128)S(1)} collective-permute-done((f32[2,128,256]{2,1,0:T(8,128)}, f32[2,128,256]{2,1,0:T(8,128)S(1)}, u32[]{:S(2)}, u32[]{:S(2)}) %collective-permute-start.1) | collective-permute-done | bytes 262176 | tf_op jit(solution)/shard_map/ppermute | solution.py:29
  9.0 1.0 fusion.28
  10.0 4.2 %collective-permute-start.2 = (f32[2,384,128]{2,1,0:T(8,128)}, f32[2,384,128]{2,1,0:T(8,128)}, u32[]{:S(2)}, u32[]{:S(2)}) collective-permute-start(f32[2,384,128]{2,1,0:T(8,128)} %get-tuple-element.12), channel_id=1, source_target_pairs={{0,1},{2,3},{4,5},{6,7},{8,9},{10,11},{12,13},{14,15},{16,17},{18,... | collective-permute-start | bytes 1179656 | tf_op jit(solution)/shard_map/ppermute | solution.py:28
  14.2 1.3 collective-permute-start.3
  15.8 3.6 %collective-permute-done.2 = f32[2,384,128]{2,1,0:T(8,128)} collective-permute-done((f32[2,384,128]{2,1,0:T(8,128)}, f32[2,384,128]{2,1,0:T(8,128)}, u32[]{:S(2)}, u32[]{:S(2)}) %collective-permute-start.2) | collective-permute-done | bytes 393248 | tf_op jit(solution)/shard_map/ppermute | solution.py:28
  19.4 5.4 %collective-permute-done.3 = f32[2,384,128]{2,1,0:T(8,128)} collective-permute-done((f32[2,384,128]{2,1,0:T(8,128)}, f32[2,384,128]{2,1,0:T(8,128)}, u32[]{:S(2)}, u32[]{:S(2)}) %collective-permute-start.3) | collective-permute-done | bytes 393248 | tf_op jit(solution)/shard_map/ppermute | solution.py:29
  24.9 1.3 pad_maximum_fusion.refs_3_
  26.2 21.1 %scan_positions.1 = (f32[416,8,128]{2,1,0:T(8,128)}, f32[3,384,512]{2,1,0:T(8,128)}) custom-call(s32[4,2]{1,0:T(4,128)S(1)} %copy.14.refs_0_, f32[12,2,128,128]{3,2,1,0:T(8,128)S(1)} %copy-done, f32[4,128,128]{2,1,0:T(8,128)S(1)} %copy-done.7, f32[2,384,512]{2,1,0:T(8,128)S(1)} %pad_maximum_fusion.refs_3_, bf16[768,256]{1,0:T(8,128)(2,1)S(1)} %copy-done.3, ...), custom_call_target="tpu_custom_call" | custom-call | tf_op jit(solution)/shard_map/scan_positions/pallas_call | solution.py:195
  47.3 1.7 %copy-done.1 = f32[3,384,512]{2,1,0:T(8,128)S(1)} copy-done((f32[3,384,512]{2,1,0:T(8,128)S(1)}, f32[3,384,512]{2,1,0:T(8,128)}, u32[]{:S(2)}) %copy-start.1) | copy-done | bytes 2359320
  48.9 1.5 %copy-done.2 = f32[416,8,128]{2,1,0:T(8,128)S(1)} copy-done((f32[416,8,128]{2,1,0:T(8,128)S(1)}, f32[416,8,128]{2,1,0:T(8,128)}, u32[]{:S(2)}) %copy-start.2) | copy-done | bytes 1703960
  50.4 63.6 %exchange.1 = (f32[416,8,128]{2,1,0:T(8,128)S(1)}, f32[3,128,256]{2,1,0:T(8,128)S(1)}) custom-call(f32[416,8,128]{2,1,0:T(8,128)S(1)} %copy-done.2, f32[3,384,512]{2,1,0:T(8,128)S(1)} %copy-done.1), custom_call_target="tpu_custom_call" | custom-call | tf_op jit(solution)/shard_map/exchange/pallas_call | solution.py:421
  114.1 0.6 add_bitcast_fusion.1
  114.7 0.7 slice_reduce_fusion
  115.4 1.4 reshape.30
  116.8 2.4 %bitcast_add_fusion = f32[24,16384]{1,0:T(8,128)S(1)} fusion(f32[3,8,128,128]{3,2,1,0:T(8,128)S(1)} %bitcast.70, f32[24,16384]{1,0:T(8,128)} %reshape.30, f32[16384]{0:T(1024)} %add_bitcast_fusion.1), kind=kLoop, calls=%fused_computation.3 | loop fusion | flops 786432 | bytes 4784128 | tf_op jit(solution)/shard_map/add | solution.py:463
  119.2 1.5 %fusion.20 = f32[12,12]{1,0:T(8,128)S(1)} fusion(f32[24,16384]{1,0:T(8,128)S(1)} %bitcast_add_fusion), kind=kOutput, calls=%fused_computation.37 | convolution fusion | flops 28311552 | bytes 1049152 | tf_op jit(solution)/shard_map/dot_general | solution.py:240
  120.7 1.5 %fusion.11 = f32[12,12]{1,0:T(8,128)S(1)} fusion(f32[24,16384]{1,0:T(8,128)S(1)} %bitcast_add_fusion), kind=kOutput, calls=%fused_computation.28 | convolution fusion | flops 28311552 | bytes 2097728 | tf_op jit(solution)/shard_map/dot_general | solution.py:243
  122.3 1.6 %convolution_add_fusion.1 = f32[12,12]{1,0:T(8,128)S(1)} fusion(f32[12,12]{1,0:T(8,128)S(1)} %fusion.20, f32[24,16384]{1,0:T(8,128)S(1)} %bitcast_add_fusion), kind=kOutput, calls=%fused_computation.24 | convolution fusion | flops 28311696 | bytes 1057344 | tf_op jit(solution)/shard_map/dot_general | solution.py:242
  123.8 1.5 %fusion.29 = (f32[12,12]{1,0:T(8,128)S(1)}, f32[12,12]{1,0:T(8,128)S(1)}) fusion(f32[12,12]{1,0:T(8,128)S(1)} %fusion.11, f32[24,16384]{1,0:T(8,128)S(1)} %bitcast_add_fusion), kind=kOutput, calls=%fused_computation.62 | convolution fusion | flops 28311840 | bytes 2106496 | tf_op jit(solution)/shard_map/dot_general | solution.py:245
  125.3 0.7 multiply_reduce_fusion
  126.7 0.2 fusion.7
  127.0 0.2 fusion.27
  127.3 0.2 fusion.6
  127.6 0.2 fusion.30
  127.8 0.2 fusion.5
  128.1 0.2 fusion.32
  128.2 0.2 fusion.4
  128.5 0.2 fusion.34
  128.7 0.2 fusion.3
  129.0 0.2 fusion.36
  129.2 0.2 fusion.2
  129.5 0.2 fusion.38
  129.6 0.2 fusion.1
  129.9 0.2 fusion.40
  130.5 2.0 %fusion.16 = f32[12,16384]{1,0:T(8,128)} fusion(f32[24,16384]{1,0:T(8,128)S(1)} %bitcast_add_fusion, f32[24,24]{1,0:T(8,128)S(1)} %convolution_divide_fusion), kind=kOutput, calls=%fused_computation.33 | convolution fusion | flops 28311552 | bytes 1843200 | tf_op jit(solution)/shard_map/dot_general | solution.py:253
  132.5 1.0 fusion.14
  133.5 0.7 gather_fusion
  134.2 2.3 %convolution_subtract_fusion = f32[12,16384]{1,0:T(8,128)S(1)} fusion(f32[12,16384]{1,0:T(8,128)} %fusion.16, f32[24,16384]{1,0:T(8,128)S(1)} %bitcast_add_fusion, f32[24,24]{1,0:T(8,128)S(1)} %convolution_divide_fusion), kind=kOutput, calls=%fused_computation.2 | convolution fusion | flops 28508160 | bytes 2629632 | tf_op jit(solution)/shard_map/dot_general | solution.py:255
  136.5 1.2 copy.18
  137.7 1.0 convolution_add_fusion
  138.8 0.2 copy.19
  139.0 0.7 copy-done.11
  139.7 0.7 divide_add_fusion
  141.7 0.1 bitcast_bitcast_fusion
  141.9 1.4 maximum_multiply_fusion
  (41 shorter events, 1.7 us)
Async XLA Ops:
  0.6 14.8 %copy-start.12 = (s32[4,2]{0,1:T(2,128)S(1)}, s32[4,2]{0,1:T(2,128)}, u32[]{:S(2)}) copy-start(s32[4,2]{0,1:T(2,128)} %param.11) | copy-start | bytes 100
  0.6 14.9 %copy-start = (f32[12,2,128,128]{3,2,1,0:T(8,128)S(1)}, f32[12,2,128,128]{3,2,1,0:T(8,128)}, u32[]{:S(2)}) copy-start(f32[12,2,128,128]{3,2,1,0:T(8,128)} %refs_1_.1) | copy-start | bytes 4718596
  0.6 3.9 %collective-permute-start = (f32[2,128,256]{2,1,0:T(8,128)}, f32[2,128,256]{2,1,0:T(8,128)S(1)}, u32[]{:S(2)}, u32[]{:S(2)}) collective-permute-start(f32[2,128,256]{2,1,0:T(8,128)} %param.10), channel_id=1, source_target_pairs={{0,2},{2,4},{4,6},{6,8},{8,10},{10,12},{12,14},{14,16},{16,18},{18... | collective-permute-start | bytes 786440 | tf_op jit(solution)/shard_map/ppermute | solution.py:28
  3.2 5.7 %collective-permute-start.1 = (f32[2,128,256]{2,1,0:T(8,128)}, f32[2,128,256]{2,1,0:T(8,128)S(1)}, u32[]{:S(2)}, u32[]{:S(2)}) collective-permute-start(f32[2,128,256]{2,1,0:T(8,128)} %param.10), channel_id=1, source_target_pairs={{2,0},{4,2},{6,4},{8,6},{10,8},{12,10},{14,12},{16,14},{18,16},{20... | collective-permute-start | bytes 786440 | tf_op jit(solution)/shard_map/ppermute | solution.py:29
  8.9 5.2 %copy-start.8 = (f32[2,384,256]{2,1,0:T(8,128)}, f32[2,384,256]{2,1,0:T(8,128)S(1)}, u32[]{:S(2)}) copy-start(f32[2,384,256]{2,1,0:T(8,128)S(1)} %constant_dynamic-update-slice_fusion) | copy-start | bytes 2359300
  10.0 9.4 %collective-permute-start.2 = (f32[2,384,128]{2,1,0:T(8,128)}, f32[2,384,128]{2,1,0:T(8,128)}, u32[]{:S(2)}, u32[]{:S(2)}) collective-permute-start(f32[2,384,128]{2,1,0:T(8,128)} %get-tuple-element.12), channel_id=1, source_target_pairs={{0,1},{2,3},{4,5},{6,7},{8,9},{10,11},{12,13},{14,15},{16,17},{18,... | collective-permute-start | bytes 1179656 | tf_op jit(solution)/shard_map/ppermute | solution.py:28
  14.2 10.7 %collective-permute-start.3 = (f32[2,384,128]{2,1,0:T(8,128)}, f32[2,384,128]{2,1,0:T(8,128)}, u32[]{:S(2)}, u32[]{:S(2)}) collective-permute-start(f32[2,384,128]{2,1,0:T(8,128)} %get-tuple-element.13), channel_id=1, source_target_pairs={{1,0},{3,2},{5,4},{7,6},{9,8},{11,10},{13,12},{15,14},{17,16},{19,... | collective-permute-start | bytes 1179656 | tf_op jit(solution)/shard_map/ppermute | solution.py:29
  15.6 9.3 %copy-start.9 = (f32[2,384,256]{2,1,0:T(8,128)S(1)}, f32[2,384,256]{2,1,0:T(8,128)}, u32[]{:S(2)}) copy-start(f32[2,384,256]{2,1,0:T(8,128)} %copy-done.8) | copy-start | bytes 2359300
  15.7 10.4 %copy-start.3 = (bf16[768,256]{1,0:T(8,128)(2,1)S(1)}, bf16[768,256]{1,0:T(8,128)(2,1)}, u32[]{:S(2)}) copy-start(bf16[768,256]{1,0:T(8,128)(2,1)} %constant.25.clone.refs_4_) | copy-start | bytes 1179652
  15.7 10.4 %copy-start.4 = (bf16[256,768]{1,0:T(8,128)(2,1)S(1)}, bf16[256,768]{1,0:T(8,128)(2,1)}, u32[]{:S(2)}) copy-start(bf16[256,768]{1,0:T(8,128)(2,1)} %constant.26.clone.refs_5_) | copy-start | bytes 1179652
  15.8 10.4 %copy-start.5 = (bf16[256,768]{1,0:T(8,128)(2,1)S(1)}, bf16[256,768]{1,0:T(8,128)(2,1)}, u32[]{:S(2)}) copy-start(bf16[256,768]{1,0:T(8,128)(2,1)} %constant.27.clone.refs_6_) | copy-start | bytes 1179652
  15.8 10.4 %copy-start.6 = (bf16[768,256]{1,0:T(8,128)(2,1)S(1)}, bf16[768,256]{1,0:T(8,128)(2,1)}, u32[]{:S(2)}) copy-start(bf16[768,256]{1,0:T(8,128)(2,1)} %constant.28.clone.refs_7_) | copy-start | bytes 1179652
  15.8 10.4 %copy-start.7 = (f32[4,128,128]{2,1,0:T(8,128)S(1)}, f32[4,128,128]{2,1,0:T(8,128)}, u32[]{:S(2)}) copy-start(f32[4,128,128]{2,1,0:T(8,128)} %refs_2_.1) | copy-start | bytes 786436
  47.3 1.7 %copy-start.1 = (f32[3,384,512]{2,1,0:T(8,128)S(1)}, f32[3,384,512]{2,1,0:T(8,128)}, u32[]{:S(2)}) copy-start(f32[3,384,512]{2,1,0:T(8,128)} %get-tuple-element.7.refs_1_) | copy-start | bytes 7077892
  48.9 1.5 %copy-start.2 = (f32[416,8,128]{2,1,0:T(8,128)S(1)}, f32[416,8,128]{2,1,0:T(8,128)}, u32[]{:S(2)}) copy-start(f32[416,8,128]{2,1,0:T(8,128)} %get-tuple-element.6.refs_0_) | copy-start | bytes 5111812
  138.7 1.0 copy-start.11
  138.7 3.0 %copy-start.10 = (f32[2,8,128,128]{3,2,1,0:T(8,128)S(1)}, f32[2,8,128,128]{3,2,1,0:T(8,128)}, u32[]{:S(2)}) copy-start(f32[2,8,128,128]{3,2,1,0:T(8,128)} %copy.18) | copy-start | bytes 3145732

commit v3 on v2

--- a/solution.py
+++ b/solution.py
@@ -16,19 +16,6 @@
 object_reg = 0.5
 probe_reg = 1.0
 total_eps = 1e-06
-
-
-def extended_2(array, sides, width):
-    for axis, dim in sides:
-        size, length = (lax.axis_size(axis), array.shape[dim])
-        up = [(i, (i + 1) % size) for i in range(size - 1)]
-        down = [(j, i) for i, j in up]
-        last = lax.slice_in_dim(array, length - width, length, axis=dim)
-        first = lax.slice_in_dim(array, 0, width, axis=dim)
-        before = lax.ppermute(last, axis, up)
-        after = lax.ppermute(first, axis, down)
-        array = jnp.concatenate([before, array, after], axis=dim)
-    return array
 
 
 def dft_tables(detector):
@@ -440,12 +427,81 @@
     )(packed, frame)
 
 
+def halo_kernel(specimen, out, *rest):
+    slots = rest[:8]
+    send_sem, recv_sem = rest[8:]
+    block_rows, block_cols = specimen.shape[1:]
+    det = (out.shape[1] - block_rows) // 2
+    here = {axis: lax.axis_index(axis) for axis in ("scan", "tile")}
+    sizes = {axis: lax.axis_size(axis) for axis in ("scan", "tile")}
+
+    def edge(shift, block):
+        low = {-1: 0, 0: 0, 1: block - det}[shift]
+        return pl.ds(low, block if shift == 0 else det)
+
+    def outer(shift, block):
+        low = {-1: det + block, 0: det, 1: 0}[shift]
+        return pl.ds(low, block if shift == 0 else det)
+
+    def valid(shift_rows, shift_cols):
+        row, col = here["scan"] + shift_rows, here["tile"] + shift_cols
+        return (row >= 0) & (row < sizes["scan"]) & (col >= 0) & (col < sizes["tile"])
+
+    def send(index):
+        shift_rows, shift_cols = directions()[index]
+        return pltpu.make_async_remote_copy(
+            src_ref=specimen.at[:, edge(shift_rows, block_rows), edge(shift_cols, block_cols)],
+            dst_ref=slots[index],
+            send_sem=send_sem.at[index],
+            recv_sem=recv_sem.at[index],
+            device_id={
+                "scan": (here["scan"] + shift_rows + sizes["scan"]) % sizes["scan"],
+                "tile": (here["tile"] + shift_cols + sizes["tile"]) % sizes["tile"],
+            },
+            device_id_type=pl.DeviceIdType.MESH,
+        )
+
+    for index, shifts in enumerate(directions()):
+        @pl.when(valid(*shifts))
+        def _():
+            send(index).start()
+    out[...] = jnp.zeros_like(out)
+    out[:, det : det + block_rows, det : det + block_cols] = specimen[...]
+    for index, (shift_rows, shift_cols) in enumerate(directions()):
+        @pl.when(valid(shift_rows, shift_cols))
+        def _():
+            send(index).wait_send()
+
+        @pl.when(valid(-shift_rows, -shift_cols))
+        def _():
+            send(index).wait_recv()
+            out[:, outer(shift_rows, block_rows), outer(shift_cols, block_cols)] = slots[index][...]
+
+
+def with_halo(specimen, det):
+    channels, block_rows, block_cols = specimen.shape
+    vmem = pl.BlockSpec(memory_space=pltpu.VMEM)
+    slots = [
+        pltpu.VMEM((channels, det if i else block_rows, det if j else block_cols), jnp.float32)
+        for i, j in directions()
+    ]
+    return pl.pallas_call(
+        halo_kernel,
+        name="halo",
+        out_shape=jax.ShapeDtypeStruct((channels, block_rows + 2 * det, block_cols + 2 * det), jnp.float32),
+        in_specs=[vmem],
+        out_specs=vmem,
+        scratch_shapes=[*slots, pltpu.SemaphoreType.DMA((8,)), pltpu.SemaphoreType.DMA((8,))],
+        compiler_params=pltpu.CompilerParams(has_side_effects=True, vmem_limit_bytes=16 * 1024 * 1024),
+    )(specimen)
+
+
 def body(probe_modes, patterns, specimen, offsets):
     detector = probe_modes.shape[-1]
     mode_count = probe_modes.shape[0]
     block_rows = specimen.shape[1]
     block_cols = specimen.shape[2]
-    extended = extended_2(specimen, (("scan", 1), ("tile", 2)), detector)
+    extended = with_halo(specimen, detector)
     packed, frame_sum = scan_positions(
         offsets, probe_modes, patterns, extended, block_rows, block_cols
     )

time: 144 us -> 135 us (0.938)
  Pallas kernels: 84.7 us -> 97.2 us
  waiting for transfers between devices: 12.5 us -> 0 us
  starting transfers between devices: 9.31 us -> 0 us
  local copies, waits for them, and re-layouts: 9.9 us -> 16.1 us
  other arithmetic: 7.8 us -> 4.39 us
  matrix products: 16.1 us -> 13.9 us
    pallas_call x0 -> x1, Pallas kernels: none -> 16.6 us  [with_halo(): pl.pallas_call(halo_kernel, name='halo', out_shape=jax.ShapeDtypeStruct((...]
    ppermute x4 -> x0, waiting for transfers between devices: 12.5 us -> none  [the longest x2 8.82 us: extended_2(): after = lax.ppermute(first, axis, down)]
    ppermute x4 -> x0, starting transfers between devices: 9.31 us -> none  [the longest x2 6.73 us: extended_2(): before = lax.ppermute(last, axis, up)]
    unnamed x31 -> x29, local copies, waits for them, and re-layouts: 6.34 us -> 11.4 us
    pallas_call x1, Pallas kernels: 63.6 us -> 58.6 us  [exchange(): pl.pallas_call(kernel, name='exchange', out_shape=(jax.ShapeDtypeStruct(p...]
    add x2, other arithmetic: 3.01 us -> 0.97 us  [body(): updated = probe_rows + grad_total / (light_total + probe_reg)]
  transfers between devices with their start and end apart: 4 -> 0, of which waited for: 3 -> 0; matrix products, arithmetic and copies ran while one was open for 1% -> 0% of each run, Pallas kernels for 0% -> 0%
where the time goes in v3:
time: 135 us; the launch traced here: 134 us
  Pallas kernels  97.2 us (72%)
  local copies, waits for them, and re-layouts  16.1 us (12%)
  matrix products  13.9 us (10%)
  other arithmetic  4.39 us (3%)
  between operations  2.94 us (2%)
    pallas_call x1, Pallas kernels, exchange(): pl.pallas_call(kernel, name='exchange', out_shape=(jax.ShapeDtypeStruct(p...  58.6 us
    pallas_call x1, Pallas kernels, scan_positions(): pl.pallas_call(kernel, name='scan_positions', out_shape=(jax.ShapeDtypeSt...  22 us
    pallas_call x1, Pallas kernels, with_halo(): pl.pallas_call(halo_kernel, name='halo', out_shape=jax.ShapeDtypeStruct((...  16.6 us
    unnamed x29, local copies, waits for them, and re-layouts  11.4 us

profile of v3, /device:TPU:0, one launch (start us, length us, event | category | flops | bytes accessed | tf_op | source)
XLA Modules:
  0.0 134.5 jit_solution(5606588082826779543)
XLA Ops:
  0.7 1.1 copy-done.3
  1.7 16.6 %halo.1.refs_3_ = f32[2,384,512]{2,1,0:T(8,128)S(1)} custom-call(f32[2,128,256]{2,1,0:T(8,128)S(1)} %copy-done.3), custom_call_target="tpu_custom_call" | custom-call | tf_op jit(solution)/shard_map/halo/pallas_call | solution.py:488
  18.3 0.8 copy.14.refs_0_
  19.1 1.0 copy-done.5
  20.0 1.0 copy-done.6
  21.0 1.0 copy-done.7
  22.0 1.0 copy-done.8
  23.0 22.0 %scan_positions.1 = (f32[416,8,128]{2,1,0:T(8,128)}, f32[3,384,512]{2,1,0:T(8,128)}) custom-call(s32[4,2]{1,0:T(4,128)S(1)} %copy.14.refs_0_, f32[12,2,128,128]{3,2,1,0:T(8,128)S(1)} %copy-done, f32[4,128,128]{2,1,0:T(8,128)S(1)} %copy-done.11, f32[2,384,512]{2,1,0:T(8,128)S(1)} %halo.1.refs_3_, bf16[768,256]{1,0:T(8,128)(2,1)S(1)} %copy-done.5, ...), custom_call_target="tpu_custom_call" | custom-call | tf_op jit(solution)/shard_map/scan_positions/pallas_call | solution.py:182
  45.0 1.7 %copy-done.1 = f32[3,384,512]{2,1,0:T(8,128)S(1)} copy-done((f32[3,384,512]{2,1,0:T(8,128)S(1)}, f32[3,384,512]{2,1,0:T(8,128)}, u32[]{:S(2)}) %copy-start.1) | copy-done | bytes 2359320
  46.7 1.5 %copy-done.2 = f32[416,8,128]{2,1,0:T(8,128)S(1)} copy-done((f32[416,8,128]{2,1,0:T(8,128)S(1)}, f32[416,8,128]{2,1,0:T(8,128)}, u32[]{:S(2)}) %copy-start.2) | copy-done | bytes 1703960
  48.1 58.6 %exchange.1 = (f32[416,8,128]{2,1,0:T(8,128)S(1)}, f32[3,128,256]{2,1,0:T(8,128)S(1)}) custom-call(f32[416,8,128]{2,1,0:T(8,128)S(1)} %copy-done.2, f32[3,384,512]{2,1,0:T(8,128)S(1)} %copy-done.1), custom_call_target="tpu_custom_call" | custom-call | tf_op jit(solution)/shard_map/exchange/pallas_call | solution.py:408
  106.8 0.7 copy-done.9
  107.5 1.2 slice.32
  108.8 2.6 %reshape.30 = f32[24,16384]{1,0:T(8,128)} reshape(f32[384,8,128]{2,1,0:T(8,128)} %slice.32) | data formatting | bytes 3145728 | tf_op jit(solution)/shard_map/reshape | solution.py:512
  111.5 1.3 copy-done.12
  112.7 1.0 bitcast_add_fusion
  113.7 1.5 %fusion.11 = f32[12,12]{1,0:T(8,128)S(1)} fusion(f32[24,16384]{1,0:T(8,128)S(1)} %bitcast_add_fusion), kind=kOutput, calls=%fused_computation.27 | convolution fusion | flops 28311552 | bytes 2097728 | tf_op jit(solution)/shard_map/dot_general | solution.py:230
  115.2 1.5 %fusion.28 = (f32[12,12]{1,0:T(8,128)S(1)}, f32[12,12]{1,0:T(8,128)S(1)}) fusion(f32[12,12]{1,0:T(8,128)S(1)} %fusion.11, f32[24,16384]{1,0:T(8,128)S(1)} %bitcast_add_fusion), kind=kOutput, calls=%fused_computation.57 | convolution fusion | flops 28311840 | bytes 2106496 | tf_op jit(solution)/shard_map/dot_general | solution.py:232
  116.7 1.5 %fusion.20 = f32[12,12]{1,0:T(8,128)S(1)} fusion(f32[24,16384]{1,0:T(8,128)S(1)} %bitcast_add_fusion), kind=kOutput, calls=%fused_computation.36 | convolution fusion | flops 28311552 | bytes 1049152 | tf_op jit(solution)/shard_map/dot_general | solution.py:227
  118.3 1.6 %convolution_add_fusion.1 = f32[12,12]{1,0:T(8,128)S(1)} fusion(f32[12,12]{1,0:T(8,128)S(1)} %fusion.20, f32[24,16384]{1,0:T(8,128)S(1)} %bitcast_add_fusion), kind=kOutput, calls=%fused_computation.23 | convolution fusion | flops 28311696 | bytes 1057344 | tf_op jit(solution)/shard_map/dot_general | solution.py:229
  119.9 0.7 multiply_reduce_fusion
  121.2 0.2 fusion.7
  121.5 0.2 fusion.27
  121.8 0.2 fusion.6
  122.0 0.1 fusion.30
  122.1 0.2 fusion.29
  122.3 0.2 fusion.5
  122.6 0.2 fusion.31
  122.7 0.2 fusion.4
  123.0 0.2 fusion.33
  123.2 0.2 fusion.3
  123.5 0.2 fusion.35
  123.7 0.2 fusion.2
  123.8 0.1 fusion.38
  124.0 0.2 fusion.37
  124.1 0.2 fusion.1
  124.4 0.2 fusion.39
  124.6 0.2 fusion
  125.0 1.1 fusion.16
  126.0 1.0 convolution_subtract_fusion
  127.1 0.2 copy.18
  127.3 1.0 fusion.14
  128.3 1.0 convolution_add_fusion
  129.4 0.2 copy.19
  129.7 0.7 gather_fusion
  130.4 0.6 slice_reduce_fusion
  132.4 1.4 %maximum_multiply_fusion = f32[12,2,128,128]{3,2,1,0:T(8,128)} fusion(f32[12,1,128,128]{3,2,1,0:T(8,128)S(1)} %get-tuple-element.14, f32[12,1,128,128]{3,2,1,0:T(8,128)S(1)} %get-tuple-element.15, f32[12]{0:T(128)S(1)} %multiply_sqrt_fusion), kind=kLoop, calls=%fused_computation.4 | loop fusion | flops 786432 | bytes 3145776 | tf_op jit(solution)/shard_map/mul | solution.py:247
  133.7 0.7 divide_add_fusion
  (29 shorter events, 1.1 us)
Async XLA Ops:
  0.6 18.4 %copy-start = (f32[12,2,128,128]{3,2,1,0:T(8,128)S(1)}, f32[12,2,128,128]{3,2,1,0:T(8,128)}, u32[]{:S(2)}) copy-start(f32[12,2,128,128]{3,2,1,0:T(8,128)} %refs_1_.1) | copy-start | bytes 4718596
  0.6 1.1 copy-start.3
  1.7 17.3 %copy-start.11 = (f32[4,128,128]{2,1,0:T(8,128)S(1)}, f32[4,128,128]{2,1,0:T(8,128)}, u32[]{:S(2)}) copy-start(f32[4,128,128]{2,1,0:T(8,128)} %refs_2_.1) | copy-start | bytes 786436
  19.0 1.0 copy-start.5
  20.0 1.0 copy-start.6
  21.0 1.0 copy-start.7
  22.0 1.0 copy-start.8
  45.0 1.7 %copy-start.1 = (f32[3,384,512]{2,1,0:T(8,128)S(1)}, f32[3,384,512]{2,1,0:T(8,128)}, u32[]{:S(2)}) copy-start(f32[3,384,512]{2,1,0:T(8,128)} %get-tuple-element.7.refs_1_) | copy-start | bytes 7077892
  46.7 1.5 %copy-start.2 = (f32[416,8,128]{2,1,0:T(8,128)S(1)}, f32[416,8,128]{2,1,0:T(8,128)}, u32[]{:S(2)}) copy-start(f32[416,8,128]{2,1,0:T(8,128)} %get-tuple-element.6.refs_0_) | copy-start | bytes 5111812
  106.8 0.7 copy-start.9
  111.3 1.4 %copy-start.12 = (f32[24,16384]{1,0:T(8,128)S(1)}, f32[24,16384]{1,0:T(8,128)}, u32[]{:S(2)}) copy-start(f32[24,16384]{1,0:T(8,128)} %reshape.30) | copy-start | bytes 4718596
  132.3 1.4 %copy-start.10 = (f32[3,128,256]{2,1,0:T(8,128)S(1)}, f32[3,128,256]{2,1,0:T(8,128)}, u32[]{:S(2)}) copy-start(f32[3,128,256]{2,1,0:T(8,128)} %copy-done.9) | copy-start | bytes 1179652
  132.3 1.4 %copy-start.4 = (f32[2,128,256]{2,1,0:T(8,128)S(1)}, f32[2,128,256]{2,1,0:T(8,128)}, u32[]{:S(2)}) copy-start(f32[2,128,256]{2,1,0:T(8,128)} %specimen.1) | copy-start | bytes 786436
